TPU v7x, 256 devices: a whole 4x4x8 slice. The times are simulated.
256 devices in a mesh: row: 32 (over z, x_hi, core), col: 8 (over x_lo, y).
Axes of the slice: x: 4 (x_hi: 2, x_lo: 2; x = x_hi * 2 + x_lo), y: 4, z: 8, core: 2. Of those that a mesh axis runs over, the one named last changes fastest.
Arguments:
- coefficients: float32 [2, 1, 256, 256, 256], P(None, None, 'col', 'row'), may hold values from -6 to 6
- real_bands: float32 [8, 256, 256, 256], P(None, 'col', 'row'), may hold values from -6 to 6
Outputs:
- spline_coefs: float32 [2, 1, 256, 256, 256], P(None, None, None, ('row', 'col'))
- spline_table: float32 [8, 256, 256, 256], P('col', 'row')
All inputs are finite; a program needn't handle non-finite values.
Results may differ from a plain program's by a relative error of at most 0.00007.
Values sent between devices are 32-bit elements; how exact they have to be, the bound alone decides.
No kernel may reach another device: no remote copies, remote signals or barrier semaphores. Data moves between devices by JAX's collectives and lax.ppermute only.
A program may use at most 64 MiB of HBM per device.

v0:
```python
import math

import jax
import jax.numpy as jnp
from jax import lax
from jax.sharding import PartitionSpec as P

highest = lax.Precision.HIGHEST


def cut_along(value, dim, length):
    before, after = (value.shape[:dim], value.shape[dim + 1 :])
    return jnp.moveaxis(value.reshape(*before, length, -1, *after), dim, 0)


def in_order(parts, dim):
    lengths = list(parts.shape[1:])
    lengths[dim] *= parts.shape[0]
    return jnp.moveaxis(parts, 0, dim).reshape(lengths)


def exchange_both(value, axis, axes, splits, concats):
    sizes = [lax.axis_size(a) for a in axes]
    parts = cut_along(value, splits[0], sizes[0])
    parts = jnp.moveaxis(cut_along(parts, splits[1] + 1, sizes[1]), 0, 1)
    inside = parts.shape[2:]
    parts = parts.reshape(-1, *inside)
    parts = lax.all_to_all(parts, axis, split_axis=0, concat_axis=0, tiled=True)
    parts = in_order(parts.reshape(*sizes, *inside), concats[0] + 1)
    return in_order(parts, concats[1])


def dft_tables(length):
    counter = jnp.arange(length, dtype=jnp.int32)
    phase = (counter[:, None] * counter[None, :] % length).astype(jnp.float32)
    angle = phase * (2.0 * math.pi / length)
    spread = counter.astype(jnp.float32) * (2.0 * math.pi / length)
    weight = 6.0 / ((4.0 + 2.0 * jnp.cos(spread)) * math.sqrt(length))
    return (jnp.cos(angle) * weight[:, None], jnp.sin(angle) * weight[:, None])


def apply_complex(stacked, tables, form):
    cosine, sine_table = tables

    def single(left, right):
        return jnp.einsum(form, left, right, precision=highest)

    real_part = single(stacked[0], cosine) - single(stacked[1], sine_table)
    imag_part = single(stacked[0], sine_table) + single(stacked[1], cosine)
    return jnp.stack([real_part, imag_part])


def local(coefficients, real_bands):
    rows = lax.axis_size("row")
    cols = lax.axis_size("col")
    z_local = coefficients.shape[2]
    y_local = coefficients.shape[3]
    x_length = coefficients.shape[4]
    z_full = z_local * cols
    y_full = y_local * rows
    x_tables = dft_tables(x_length)
    y_tables = dft_tables(y_full)
    z_tables = dft_tables(z_full)
    turned = jnp.transpose(real_bands, (0, 3, 2, 1))
    by_band = lax.all_to_all(turned, "col", split_axis=0, concat_axis=3, tiled=True)
    spline_table = lax.all_to_all(by_band, "row", split_axis=1, concat_axis=2, tiled=True)
    first = apply_complex(coefficients, x_tables, "bzyk,kx->bzxy")
    planes = exchange_both(first, ("row", "col"), ("row", "col"), (3, 3), (4, 2))
    along_second = apply_complex(planes, y_tables, "bzxk,kn->bzxn")
    spline_coefs = apply_complex(along_second, z_tables, "bkxy,kn->bnxy")
    return (spline_coefs, spline_table)


def solution(mesh):
    placed = (P(None, None, "col", "row", None), P(None, "col", "row", None))
    return jax.shard_map(
        local,
        mesh=mesh,
        in_specs=placed,
        out_specs=(P(None, None, None, ("row", "col"), None), P("col", "row", None, None)),
        check_vma=False,
    )
```

profile of v0, /device:TPU:8, one launch (start us, length us, event | category | flops | bytes accessed | tf_op | source)
XLA Modules:
  0.0 126.3 jit_solution(6393494402491808172)
XLA Ops:
  0.6 3.5 %copy.56 = f32[8,32,8,256]{3,1,2,0:T(8,128)} copy(f32[8,32,8,256]{3,2,1,0:T(8,128)} %param.3) | data formatting | bytes 4194304 | tf_op args[1]
  4.2 0.0 copy-start
  4.2 6.5 %all-to-all-start.1 = ((f32[8,256,8,32]{1,3,2,0:T(8,128)}), f32[8,256,8,32]{1,3,2,0:T(8,128)}, u32[]{:S(2)}, u32[]{:S(2)}) async-start(f32[8,256,8,32]{1,3,2,0:T(8,128)} %bitcast.72), calls=%async_computation.1 | async-start | bytes 4194304 | tf_op jit(solution)/shard_map/all_to_all | solution.py:65
  10.7 0.0 copy-done
  10.8 1.4 %fusion.7 = f32[256,32,8]{0,1,2:T(8,128)S(1)} fusion(f32[1,1,32,8,256]{4,3,2,1,0:T(8,128)S(1)} %get-tuple-element.13, f32[256]{0:T(256)S(1)} %multiply_divide_fusion), kind=kOutput, calls=%fused_computation.23 | convolution fusion | flops 202309632 | bytes 525312 | tf_op jit(solution)/shard_map/bzyk,kx->bzxy/dot_general | solution.py:46
  12.2 1.4 %fusion.2 = f32[1,32,256,8]{2,1,3,0:T(8,128)S(1)} fusion(f32[256,32,8]{0,1,2:T(8,128)S(1)} %fusion.7, f32[1,1,32,8,256]{4,3,2,1,0:T(8,128)S(1)} %get-tuple-element.12, f32[256]{0:T(256)S(1)} %multiply_divide_fusion), kind=kOutput, calls=%fused_computation.11 | convolution fusion | flops 202375168 | bytes 787456 | tf_op jit(solution)/shard_map/bzyk,kx->bzxy/dot_general | solution.py:46
  13.6 0.4 copy.30
  14.0 1.4 %fusion.11 = f32[256,32,8]{0,1,2:T(8,128)S(1)} fusion(f32[1,1,32,8,256]{4,3,2,1,0:T(8,128)S(1)} %get-tuple-element.13, f32[256]{0:T(256)S(1)} %multiply_divide_fusion), kind=kOutput, calls=%fused_computation.27 | convolution fusion | flops 202309632 | bytes 525312 | tf_op jit(solution)/shard_map/bzyk,kx->bzxy/dot_general | solution.py:46
  15.4 1.4 %fusion.3 = f32[1,32,256,8]{2,1,3,0:T(8,128)S(1)} fusion(f32[256,32,8]{0,1,2:T(8,128)S(1)} %fusion.11, f32[1,1,32,8,256]{4,3,2,1,0:T(8,128)S(1)} %get-tuple-element.12, f32[256]{0:T(256)S(1)} %multiply_divide_fusion), kind=kOutput, calls=%fused_computation.13 | convolution fusion | flops 202375168 | bytes 787456 | tf_op jit(solution)/shard_map/bzyk,kx->bzxy/dot_general | solution.py:46
  16.8 0.4 copy.29
  17.3 0.2 pad_maximum_fusion
  17.5 0.2 copy.58
  17.7 1.7 %reshape.102 = f32[256,1,512]{2,1,0:T(1,128)} reshape(f32[256,1,1,2,8,32]{5,4,3,2,1,0:T(8,128)S(1)} %bitcast.75) | data formatting | bytes 1048576
  19.4 15.7 %all-to-all-done.1 = f32[8,256,8,32]{1,3,2,0:T(8,128)} async-done(((f32[8,256,8,32]{1,3,2,0:T(8,128)}), f32[8,256,8,32]{1,3,2,0:T(8,128)}, u32[]{:S(2)}, u32[]{:S(2)}) %all-to-all-start.1) | async-done | bytes 2097184 | tf_op jit(solution)/shard_map/all_to_all | solution.py:65
  35.1 13.7 %all-to-all-start = ((f32[256,1,512]{2,1,0:T(1,128)}), f32[256,1,512]{2,1,0:T(1,128)S(1)}, u32[]{:S(2)}, u32[]{:S(2)}) async-start(f32[256,1,512]{2,1,0:T(1,128)} %reshape.102), calls=%async_computation | async-start | bytes 1048576 | tf_op jit(solution)/shard_map/all_to_all | solution.py:28
  48.8 1.7 %copy.37 = f32[8,256,8,32]{1,3,0,2:T(8,128)S(1)} copy(f32[8,256,8,32]{1,3,2,0:T(8,128)} %all-to-all-done.1) | data formatting | bytes 4194304 | tf_op jit(solution)/shard_map/all_to_all | solution.py:65
  50.6 2.0 %copy.38 = f32[1,256,8,256]{3,2,0,1:T(8,128)} copy(f32[1,256,8,256]{1,3,2,0:T(8,128)S(1)} %bitcast.79) | data formatting | bytes 4194304 | tf_op jit(solution)/shard_map/all_to_all | solution.py:65
  52.5 15.4 %all-to-all-done = f32[256,1,512]{2,1,0:T(1,128)S(1)} async-done(((f32[256,1,512]{2,1,0:T(1,128)}), f32[256,1,512]{2,1,0:T(1,128)S(1)}, u32[]{:S(2)}, u32[]{:S(2)}) %all-to-all-start) | async-done | bytes 524320 | tf_op jit(solution)/shard_map/all_to_all | solution.py:28
  68.0 5.1 %all-to-all-start.2 = ((f32[1,256,8,256]{3,2,0,1:T(8,128)}), f32[1,256,8,256]{3,2,0,1:T(8,128)}, u32[]{:S(2)}, u32[]{:S(2)}) async-start(f32[1,256,8,256]{3,2,0,1:T(8,128)} %copy.38), calls=%async_computation.2 | async-start | bytes 4194304 | tf_op jit(solution)/shard_map/all_to_all | solution.py:66
  73.1 0.5 broadcast.108
  73.6 1.9 %reduce = f32[256,512]{1,0:T(8,128)S(1)} reduce(f32[256,1,512]{2,1,0:T(1,128)S(1)} %all-to-all-done, f32[]{:T(128)} %broadcast.108), dimensions={1}, to_apply=%all_to_all.29.reduce_sub_computation | reduce | bytes 1048580 | tf_op jit(solution)/shard_map/all_to_all | solution.py:28
  75.5 0.5 reshape.103
  76.1 0.2 copy.57
  76.3 0.2 fusion.68
  76.5 0.3 copy.35
  76.8 0.3 copy.34
  77.1 1.4 %fusion.18 = f32[256,256]{1,0:T(8,128)S(1)} fusion(f32[256,256]{1,0:T(8,128)S(1)} %bitcast.85, f32[256]{0:T(256)S(1)} %multiply_divide_fusion), kind=kOutput, calls=%fused_computation.36 | convolution fusion | flops 202309632 | bytes 525312 | tf_op jit(solution)/shard_map/bzxk,kn->bzxn/dot_general | solution.py:46
  78.5 1.4 %fusion.17 = f32[256,256]{1,0:T(8,128)S(1)} fusion(f32[256,256]{1,0:T(8,128)S(1)} %bitcast.86, f32[256]{0:T(256)S(1)} %multiply_divide_fusion), kind=kOutput, calls=%fused_computation.35 | convolution fusion | flops 202309632 | bytes 525312 | tf_op jit(solution)/shard_map/bzxk,kn->bzxn/dot_general | solution.py:46
  79.8 1.4 %convolution_subtract_fusion.1 = f32[256,256]{1,0:T(8,128)S(1)} fusion(f32[256,256]{1,0:T(8,128)S(1)} %fusion.17, f32[256,256]{1,0:T(8,128)S(1)} %bitcast.83, f32[256]{0:T(256)S(1)} %multiply_divide_fusion), kind=kOutput, calls=%fused_computation.9 | convolution fusion | flops 202375168 | bytes 787456 | tf_op jit(solution)/shard_map/bzxk,kn->bzxn/dot_general | solution.py:46
  81.2 1.5 %fusion.16 = f32[256,256]{1,0:T(8,128)S(1)} fusion(f32[256,256]{1,0:T(8,128)S(1)} %convolution_subtract_fusion.1, f32[256]{0:T(256)S(1)} %multiply_divide_fusion), kind=kOutput, calls=%fused_computation.34 | convolution fusion | flops 202309632 | bytes 525312 | tf_op jit(solution)/shard_map/bkxy,kn->bnxy/dot_general | solution.py:46
  82.7 1.4 %convolution_add_fusion.1 = f32[256,256]{1,0:T(8,128)S(1)} fusion(f32[256,256]{1,0:T(8,128)S(1)} %fusion.18, f32[256,256]{1,0:T(8,128)S(1)} %bitcast.84, f32[256]{0:T(256)S(1)} %multiply_divide_fusion), kind=kOutput, calls=%fused_computation.8 | convolution fusion | flops 202375168 | bytes 787456 | tf_op jit(solution)/shard_map/bzxk,kn->bzxn/dot_general | solution.py:46
  84.1 1.5 %fusion.1 = f32[1,1,256,1,256]{4,2,3,1,0:T(8,128)S(1)} fusion(f32[256,256]{1,0:T(8,128)S(1)} %fusion.16, f32[256,256]{1,0:T(8,128)S(1)} %convolution_add_fusion.1, f32[256]{0:T(256)S(1)} %multiply_divide_fusion), kind=kOutput, calls=%fused_computation.7 | convolution fusion | flops 202375168 | bytes 787456 | tf_op jit(solution)/shard_map/bkxy,kn->bnxy/dot_general | solution.py:46
  85.6 1.7 %fusion.19 = f32[256,256]{1,0:T(8,128)S(1)} fusion(f32[256,256]{1,0:T(8,128)S(1)} %convolution_subtract_fusion.1, f32[256]{0:T(256)S(1)} %multiply_divide_fusion), kind=kOutput, calls=%fused_computation.37 | convolution fusion | flops 202309632 | bytes 525312 | tf_op jit(solution)/shard_map/bkxy,kn->bnxy/dot_general | solution.py:46
  87.4 1.5 %fusion = f32[1,1,256,1,256]{4,2,3,1,0:T(8,128)S(1)} fusion(f32[256,256]{1,0:T(8,128)S(1)} %fusion.19, f32[256,256]{1,0:T(8,128)S(1)} %convolution_add_fusion.1, f32[256]{0:T(256)S(1)} %multiply_divide_fusion), kind=kOutput, calls=%fused_computation.5 | convolution fusion | flops 202375168 | bytes 787456 | tf_op jit(solution)/shard_map/bkxy,kn->bnxy/dot_general | solution.py:46
  88.9 1.3 %copy.40 = f32[2,1,256,1,256]{4,3,2,1,0:T(1,128)} copy(f32[2,1,256,1,256]{4,2,3,1,0:T(8,128)S(1)} %pad_maximum_fusion.1) | data formatting | bytes 1048576
  90.3 33.0 %all-to-all-done.2 = f32[1,256,8,256]{3,2,0,1:T(8,128)} async-done(((f32[1,256,8,256]{3,2,0,1:T(8,128)}), f32[1,256,8,256]{3,2,0,1:T(8,128)}, u32[]{:S(2)}, u32[]{:S(2)}) %all-to-all-start.2) | async-done | bytes 2097184 | tf_op jit(solution)/shard_map/all_to_all | solution.py:66
  123.2 3.1 %copy.55 = f32[1,8,32,8,256]{4,3,2,1,0:T(8,128)} copy(f32[1,8,32,8,256]{4,3,1,2,0:T(8,128)} %bitcast.28) | data formatting | bytes 4194304 | tf_op jit(solution)/shard_map/all_to_all | solution.py:66
  (3 shorter events, 0.1 us)
Async XLA Ops:
  4.2 6.6 %copy-start = (f32[2,1,32,8,256]{4,3,2,1,0:T(8,128)S(1)}, f32[2,1,32,8,256]{4,3,2,1,0:T(8,128)}, u32[]{:S(2)}) copy-start(f32[2,1,32,8,256]{4,3,2,1,0:T(8,128)} %param.2) | copy-start | bytes 1572868
  4.2 30.9 %all-to-all-start.1 = ((f32[8,256,8,32]{1,3,2,0:T(8,128)}), f32[8,256,8,32]{1,3,2,0:T(8,128)}, u32[]{:S(2)}, u32[]{:S(2)}) async-start(f32[8,256,8,32]{1,3,2,0:T(8,128)} %bitcast.72), calls=%async_computation.1 | async-start | bytes 4194304 | tf_op jit(solution)/shard_map/all_to_all | solution.py:65
  35.1 32.8 %all-to-all-start = ((f32[256,1,512]{2,1,0:T(1,128)}), f32[256,1,512]{2,1,0:T(1,128)S(1)}, u32[]{:S(2)}, u32[]{:S(2)}) async-start(f32[256,1,512]{2,1,0:T(1,128)} %reshape.102), calls=%async_computation | async-start | bytes 1048576 | tf_op jit(solution)/shard_map/all_to_all | solution.py:28
  68.0 55.3 %all-to-all-start.2 = ((f32[1,256,8,256]{3,2,0,1:T(8,128)}), f32[1,256,8,256]{3,2,0,1:T(8,128)}, u32[]{:S(2)}, u32[]{:S(2)}) async-start(f32[1,256,8,256]{3,2,0,1:T(8,128)} %copy.38), calls=%async_computation.2 | async-start | bytes 4194304 | tf_op jit(solution)/shard_map/all_to_all | solution.py:66
where the time goes:
time: 129 us; the launch traced here: 126 us
  waiting for transfers between devices  64.1 us (50%)
  starting transfers between devices  25.3 us (20%)
  matrix products  17.4 us (13%)
  local copies, waits for them, and re-layouts  16.5 us (13%)
  other arithmetic  2.19 us (2%)
    all_to_all x1, waiting for transfers between devices, local(): lax.all_to_all(by_band, 'row', split_axis=1, concat_axis=2, tiled=True)  33 us
    dot_general x12, matrix products, single(): return jnp.einsum(form, left, right, precision=highest)  17.4 us
    all_to_all x1, waiting for transfers between devices, local(): lax.all_to_all(turned, 'col', split_axis=0, concat_axis=3, tiled=True)  15.7 us
    all_to_all x1, waiting for transfers between devices, exchange_both(): parts = lax.all_to_all(parts, axis, split_axis=0, concat_axis=0, tiled=True)  15.4 us
    all_to_all x1, starting transfers between devices, exchange_both(): parts = lax.all_to_all(parts, axis, split_axis=0, concat_axis=0, tiled=True)  13.7 us
    unnamed x6, local copies, waits for them, and re-layouts  7.13 us
    all_to_all x1, starting transfers between devices, local(): lax.all_to_all(turned, 'col', split_axis=0, concat_axis=3, tiled=True)  6.51 us
    all_to_all x1, starting transfers between devices, local(): lax.all_to_all(by_band, 'row', split_axis=1, concat_axis=2, tiled=True)  5.13 us
  transfers between devices with their start and end apart: 3, of which 3 were waited for; matrix products, arithmetic and copies ran while one was open for 23% of the time, Pallas kernels for 0%

commit v1 on v0

v1 whole, which is shorter than its diff:
```python
import functools

import jax
import jax.numpy as jnp
import ml_dtypes
import numpy as np
from jax import lax
from jax.experimental import pallas as pl
from jax.experimental.pallas import tpu as pltpu
from jax.sharding import PartitionSpec as P

N = 256
ROWS, COLS = 32, 8
ZL, YL, XL = N // COLS, N // ROWS, N // ROWS
BANDS = 8
PIECE = 20
LANES = 128
f32 = jnp.float32
bf16 = jnp.bfloat16


@functools.cache
def tables():
    k = np.arange(N)
    angle = 2.0 * np.pi * ((k[:, None] * k[None, :]) % N) / N
    weight = 6.0 / ((4.0 + 2.0 * np.cos(2.0 * np.pi * k / N)) * np.sqrt(N))
    both = np.concatenate([np.cos(angle) * weight[None, :], np.sin(angle) * weight[None, :]])
    by_rest = both.reshape(2 * N, ROWS, YL).swapaxes(1, 2).reshape(2 * N, N)
    out = []
    for whole in (both, by_rest):
        high = whole.astype(ml_dtypes.bfloat16)
        low = (whole - high.astype(np.float64)).astype(ml_dtypes.bfloat16)
        out += [high, low]
    return tuple(out)


def split(value):
    high = value.astype(bf16)
    return high, (value - high.astype(f32)).astype(bf16)


def product(w_high, w_low, value, dims):
    high, low = split(value)

    def one(left, right):
        return lax.dot_general(left, right, (dims, ((), ())), preferred_element_type=f32)

    return one(w_high, high) + (one(w_high, low) + one(w_low, high))


def exchange_blocks(vs):
    lane = lax.broadcasted_iota(jnp.int32, (8, LANES), 1)
    low = lane < 64
    even = (lane & 32) == 0
    u = list(vs)
    for i in (0, 1):
        a, b = u[i], u[i + 2]
        u[i] = jnp.where(low, a, pltpu.roll(b, 64, 1))
        u[i + 2] = jnp.where(low, pltpu.roll(a, 64, 1), b)
    for i in (0, 2):
        a, b = u[i], u[i + 1]
        u[i] = jnp.where(even, a, pltpu.roll(b, 32, 1))
        u[i + 1] = jnp.where(even, pltpu.roll(a, 96, 1), b)
    return u


def pack(coef_ref, bands_ref, wh_ref, wl_ref, out_ref, cbuf, buf, spec, sems):
    halves = [pl.ds(h * LANES, LANES) for h in range(2)]
    starts = [pltpu.make_async_copy(coef_ref.at[:, halves[h]], cbuf.at[h], sems.at[h]) for h in range(2)]
    copies = [
        [pltpu.make_async_copy(bands_ref.at[b, :, halves[h]], buf.at[b, h], sems.at[2 + 2 * b + h]) for h in range(2)]
        for b in range(BANDS)
    ]
    for copy in starts + sum(copies, []):
        copy.start()
    for copy in starts:
        copy.wait()
    rows = [
        jnp.concatenate([cbuf[h, pl.ds(part * N + y, ZL, stride=YL), :] for h in range(2)], axis=1)
        for part in range(2)
        for y in range(YL)
    ]
    q = product(wh_ref[...], wl_ref[...], jnp.concatenate(rows), ((1,), (1,)))
    for h in range(2):
        one, two = (slice(p * N + h * LANES, p * N + (h + 1) * LANES) for p in range(2))
        spec[h, pl.ds(0, N), :] = q[:N, one] - q[N:, two]
        spec[h, pl.ds(N, N), :] = q[N:, one] + q[:N, two]
    for b in range(BANDS):
        base = b * ROWS * PIECE
        for xh in range(2):
            copies[b][xh].wait()
            for yh in range(2):
                block = jnp.concatenate([buf[b, xh, pl.ds(yh * 4 + k, ZL, stride=YL), :] for k in range(4)])
                turned = block.T
                for r in range(16):
                    row = base + PIECE * (xh * 16 + r) + 8 * yh
                    out_ref[pl.ds(row, 8), :] = turned[r * 8 : r * 8 + 8]
        for part in range(2):
            for yh in range(2):
                for g in range(ROWS // 8):
                    out_ref[pl.ds(base + PIECE * 8 * g + 16 + part * 2 + yh, 8, stride=PIECE), :] = spec[
                        yh, pl.ds(part * N + g * 64 + b, 8, stride=8), :
                    ]


GROUPS = 4


def unpack(in_ref, yh_ref, yl_ref, wh_ref, wl_ref, coefs_ref, table_ref, tab, field, sems):
    flat = tab.reshape(2, XL * N, LANES)
    size = N // GROUPS
    copies = []
    for group in range(GROUPS):
        for h in range(2):
            for r in range(group * ROWS // GROUPS, (group + 1) * ROWS // GROUPS):
                for yh in range(2):
                    vs = [in_ref[pl.ds(PIECE * ((h * 4 + c) * ROWS + r) + 8 * yh, 8), :] for c in range(4)]
                    for k, v in enumerate(exchange_blocks(vs)):
                        flat[h, pl.ds(r * YL + yh * 4 + k, XL, stride=N), :] = v
            where = pl.ds(group * size, size)
            copies.append(
                pltpu.make_async_copy(
                    tab.at[h, :, where, :],
                    table_ref.at[:, where, pl.ds(h * LANES, LANES)],
                    sems.at[2 * group + h],
                )
            )
            copies[-1].start()
    for part in range(2):
        for yh in range(2):
            for g in range(ROWS // 8):
                for h in range(2):
                    vs = [
                        in_ref[
                            pl.ds(PIECE * ((h * 4 + c) * ROWS + g * 8) + 16 + part * 2 + yh, 8, stride=PIECE), :
                        ]
                        for c in range(4)
                    ]
                    for k, v in enumerate(exchange_blocks(vs)):
                        field[pl.ds((yh * 4 + k) * ROWS + g * 8, 8), pl.ds(part * N + h * LANES, LANES)] = v
    q = product(yh_ref[...], yl_ref[...], field[...], ((1,), (0,)))
    along = jnp.concatenate([q[:N, :N] - q[N:, N:], q[N:, :N] + q[:N, N:]])
    q = product(wh_ref[...], wl_ref[...], along, ((1,), (1,)))
    real = q[:N, :N] - q[N:, N:]
    imag = q[N:, :N] + q[:N, N:]
    for h in range(2):
        lanes = slice(h * LANES, (h + 1) * LANES)
        coefs_ref[pl.ds(h, N, stride=2), :] = real[:, lanes]
        coefs_ref[pl.ds(2 * N + h, N, stride=2), :] = imag[:, lanes]
    for copy in copies:
        copy.wait()


vmem = pl.BlockSpec(memory_space=pltpu.VMEM)
anywhere = pl.BlockSpec(memory_space=pltpu.HBM)


def local(coefficients, real_bands):
    assert coefficients.shape == (2, 1, ZL, YL, N)
    assert real_bands.shape == (BANDS, ZL, YL, N)
    assert (lax.axis_size("row"), lax.axis_size("col")) == (ROWS, COLS)
    wh, wl, yh, yl = (jnp.asarray(t) for t in tables())
    total = ROWS * COLS * PIECE
    packed = pl.pallas_call(
        pack,
        name="pack",
        out_shape=jax.ShapeDtypeStruct((total, LANES), f32),
        in_specs=[anywhere, anywhere, vmem, vmem],
        out_specs=vmem,
        scratch_shapes=[
            pltpu.VMEM((2, 2 * ZL * YL, LANES), f32),
            pltpu.VMEM((BANDS, 2, ZL * YL, LANES), f32),
            pltpu.VMEM((2, 2 * N, LANES), f32),
            pltpu.SemaphoreType.DMA((2 + 2 * BANDS,)),
        ],
        compiler_params=pltpu.CompilerParams(vmem_limit_bytes=24 << 20),
    )(coefficients.reshape(2 * ZL * YL, N), real_bands.reshape(BANDS, ZL * YL, N), wh, wl)
    packed = packed.reshape(ROWS * COLS, PIECE // 4, 4, LANES)
    got = lax.all_to_all(packed, ("col", "row"), split_axis=0, concat_axis=0, tiled=True)
    coefs, table = pl.pallas_call(
        unpack,
        name="unpack",
        out_shape=[
            jax.ShapeDtypeStruct((4 * N, LANES), f32),
            jax.ShapeDtypeStruct((XL, N, N), f32),
        ],
        in_specs=[vmem] * 5,
        out_specs=[vmem, anywhere],
        scratch_shapes=[
            pltpu.VMEM((2, XL, N, LANES), f32),
            pltpu.VMEM((N, 2 * N), f32),
            pltpu.SemaphoreType.DMA((2 * GROUPS,)),
        ],
        compiler_params=pltpu.CompilerParams(vmem_limit_bytes=24 << 20),
    )(got.reshape(total, LANES), yh, yl, wh, wl)
    return coefs.reshape(2, 1, N, 1, N), table.reshape(1, XL, N, N)


def solution(mesh):
    placed = (P(None, None, "col", "row", None), P(None, "col", "row", None))
    return jax.shard_map(
        local,
        mesh=mesh,
        in_specs=placed,
        out_specs=(P(None, None, None, ("row", "col"), None), P("col", "row", None, None)),
        check_vma=False,
    )
```

time: 129 us -> 91.7 us (0.71); the launches traced: 126 us -> 91.5 us
  blocking collectives: 0 us -> 78.3 us
  waiting for transfers between devices: 64.1 us -> 0 us
  starting transfers between devices: 25.3 us -> 0 us
  matrix products: 17.4 us -> 0 us
  local copies, waits for them, and re-layouts: 16.5 us -> 4.55 us
  Pallas kernels: 0 us -> 7.88 us
  other arithmetic: 2.19 us -> 0 us
    all_to_all x0 -> x1, blocking collectives: none -> 78.3 us  [local(): lax.all_to_all(packed, ('col', 'row'), split_axis=0, concat_axis=0, tiled...]
    all_to_all x3 -> x0, waiting for transfers between devices: 64.1 us -> none  [the longest x1 33 us: local(): lax.all_to_all(by_band, 'row', split_axis=1, concat_axis=2, tiled=True)]
    all_to_all x3 -> x0, starting transfers between devices: 25.3 us -> none  [the longest x1 13.7 us: exchange_both(): parts = lax.all_to_all(parts, axis, split_axis=0, concat_axis=0, tiled=True)]
    dot_general x12 -> x0, matrix products: 17.4 us -> none  [single(): return jnp.einsum(form, left, right, precision=highest)]
    pallas_call x0 -> x2, Pallas kernels: none -> 7.88 us  [the longest x1 5.14 us: local(): pl.pallas_call(unpack, name='unpack', out_shape=[jax.ShapeDtypeStruct((4...]
    all_to_all x4 -> x0, local copies, waits for them, and re-layouts: 7.32 us -> none  [the longest x2 3.7 us: local(): lax.all_to_all(turned, 'col', split_axis=0, concat_axis=3, tiled=True)]
    unnamed x6 -> x16, local copies, waits for them, and re-layouts: 7.13 us -> 4.55 us
    all_to_all x1 -> x0, other arithmetic: 1.88 us -> none  [exchange_both(): parts = lax.all_to_all(parts, axis, split_axis=0, concat_axis=0, tiled=True)]
  transfers between devices with their start and end apart: 3 -> 0, of which waited for: 3 -> 0; matrix products, arithmetic and copies ran while one was open for 23% -> 0% of each run, Pallas kernels for 0% -> 0%
where the time goes in v1:
time: 91.7 us; the launch traced here: 91.5 us
  blocking collectives  78.3 us (85%)
  Pallas kernels  7.88 us (9%)
  local copies, waits for them, and re-layouts  4.55 us (5%)
    all_to_all x1, blocking collectives, local(): lax.all_to_all(packed, ('col', 'row'), split_axis=0, concat_axis=0, tiled...  78.3 us
    pallas_call x1, Pallas kernels, local(): pl.pallas_call(unpack, name='unpack', out_shape=[jax.ShapeDtypeStruct((4...  5.14 us
    unnamed x16, local copies, waits for them, and re-layouts  4.55 us
    pallas_call x1, Pallas kernels, local(): pl.pallas_call(pack, name='pack', out_shape=jax.ShapeDtypeStruct((total,...  2.74 us

profile of v1, /device:TPU:8, one launch (start us, length us, event | category | flops | bytes accessed | tf_op | source)
XLA Modules:
  0.0 91.5 jit_solution(17521326121074443532)
XLA Ops:
  0.6 0.0 copy-start
  0.6 1.6 %copy-done = f32[8,32,8,256]{3,2,1,0:T(8,128)S(1)} copy-done((f32[8,32,8,256]{3,2,1,0:T(8,128)S(1)}, f32[8,32,8,256]{3,2,1,0:T(8,128)}, u32[]{:S(2)}) %copy-start) | copy-done | bytes 2097176
  2.2 0.0 copy-start.1
  2.2 0.9 %copy-done.1 = bf16[512,256]{1,0:T(8,128)(2,1)S(1)} copy-done((bf16[512,256]{1,0:T(8,128)(2,1)S(1)}, bf16[512,256]{1,0:T(8,128)(2,1)}, u32[]{:S(2)}) %copy-start.1) | copy-done | bytes 262168
  3.2 0.0 copy-start.3
  3.2 0.9 %copy-done.3 = bf16[512,256]{1,0:T(8,128)(2,1)S(1)} copy-done((bf16[512,256]{1,0:T(8,128)(2,1)S(1)}, bf16[512,256]{1,0:T(8,128)(2,1)}, u32[]{:S(2)}) %copy-start.3) | copy-done | bytes 262168
  4.1 0.0 copy-start.5
  4.1 1.0 %copy-done.5 = f32[2,1,32,8,256]{4,3,2,1,0:T(8,128)S(1)} copy-done((f32[2,1,32,8,256]{4,3,2,1,0:T(8,128)S(1)}, f32[2,1,32,8,256]{4,3,2,1,0:T(8,128)}, u32[]{:S(2)}) %copy-start.5) | copy-done | bytes 524312
  5.2 2.7 %pack.1 = f32[5120,128]{1,0:T(8,128)S(1)} custom-call(f32[512,256]{1,0:T(8,128)S(1)} %bitcast.9, f32[8,256,256]{2,1,0:T(8,128)S(1)} %bitcast.8, bf16[512,256]{1,0:T(8,128)(2,1)S(1)} %copy-done.3, bf16[512,256]{1,0:T(8,128)(2,1)S(1)} %copy-done.1), custom_call_target="tpu_custom_call" | custom-call | tf_op jit(solution)/shard_map/pack/pallas_call | solution.py:164
  7.9 0.0 copy-start.2
  7.9 0.0 copy-start.4
  7.9 0.0 copy-start.6
  8.0 0.0 copy-start.7
  8.0 78.3 %all_to_all.5 = f32[256,5,4,128]{3,2,1,0:T(4,128)S(1)} all-to-all(f32[256,5,4,128]{3,2,1,0:T(4,128)S(1)} %bitcast.7), channel_id=1, replica_groups=mesh['row'=32,'col'=8] {'col','row'}, dimensions={0} | all-to-all | bytes 5242880 | tf_op jit(solution)/shard_map/all_to_all | solution.py:179
  86.3 0.0 copy-done.2
  86.3 0.0 copy-done.4
  86.3 0.0 copy-done.6
  86.3 0.0 copy-done.7
  86.3 5.1 %unpack.1 = (f32[1024,128]{1,0:T(8,128)}, f32[8,256,256]{2,1,0:T(8,128)}) custom-call(f32[5120,128]{1,0:T(8,128)S(1)} %bitcast.6, bf16[512,256]{1,0:T(8,128)(2,1)S(1)} %copy-done.7, bf16[512,256]{1,0:T(8,128)(2,1)S(1)} %copy-done.6, bf16[512,256]{1,0:T(8,128)(2,1)S(1)} %copy-done.4, bf16[512,256]{1,0:T(8,128)(2,1)S(1)} %copy-done.2), custom_call_target="tpu_custom_call" | custom-call | tf_op jit(solution)/shard_map/unpack/pallas_call | solution.py:180
Async XLA Ops:
  0.6 1.6 %copy-start = (f32[8,32,8,256]{3,2,1,0:T(8,128)S(1)}, f32[8,32,8,256]{3,2,1,0:T(8,128)}, u32[]{:S(2)}) copy-start(f32[8,32,8,256]{3,2,1,0:T(8,128)} %param.7) | copy-start | bytes 6291460
  2.2 0.9 %copy-start.1 = (bf16[512,256]{1,0:T(8,128)(2,1)S(1)}, bf16[512,256]{1,0:T(8,128)(2,1)}, u32[]{:S(2)}) copy-start(bf16[512,256]{1,0:T(8,128)(2,1)} %constant.9.clone.wl_ref) | copy-start | bytes 786436
  3.2 0.9 %copy-start.3 = (bf16[512,256]{1,0:T(8,128)(2,1)S(1)}, bf16[512,256]{1,0:T(8,128)(2,1)}, u32[]{:S(2)}) copy-start(bf16[512,256]{1,0:T(8,128)(2,1)} %constant.8.clone.wh_ref) | copy-start | bytes 786436
  4.1 1.0 %copy-start.5 = (f32[2,1,32,8,256]{4,3,2,1,0:T(8,128)S(1)}, f32[2,1,32,8,256]{4,3,2,1,0:T(8,128)}, u32[]{:S(2)}) copy-start(f32[2,1,32,8,256]{4,3,2,1,0:T(8,128)} %param.6) | copy-start | bytes 1572868
  7.9 78.4 %copy-start.2 = (bf16[512,256]{1,0:T(8,128)(2,1)S(1)}, bf16[512,256]{1,0:T(8,128)(2,1)}, u32[]{:S(2)}) copy-start(bf16[512,256]{1,0:T(8,128)(2,1)} %constant.9.clone.wl_ref) | copy-start | bytes 786436
  7.9 78.4 %copy-start.4 = (bf16[512,256]{1,0:T(8,128)(2,1)S(1)}, bf16[512,256]{1,0:T(8,128)(2,1)}, u32[]{:S(2)}) copy-start(bf16[512,256]{1,0:T(8,128)(2,1)} %constant.8.clone.wh_ref) | copy-start | bytes 786436
  7.9 78.4 %copy-start.6 = (bf16[512,256]{1,0:T(8,128)(2,1)S(1)}, bf16[512,256]{1,0:T(8,128)(2,1)}, u32[]{:S(2)}) copy-start(bf16[512,256]{1,0:T(8,128)(2,1)} %constant.11.clone.yl_ref) | copy-start | bytes 786436
  8.0 78.4 %copy-start.7 = (bf16[512,256]{1,0:T(8,128)(2,1)S(1)}, bf16[512,256]{1,0:T(8,128)(2,1)}, u32[]{:S(2)}) copy-start(bf16[512,256]{1,0:T(8,128)(2,1)} %constant.10.clone.yh_ref) | copy-start | bytes 786436

commit v2 on v1

v2 whole, which is shorter than its diff:
```python
import functools

import jax
import jax.numpy as jnp
import ml_dtypes
import numpy as np
from jax import lax
from jax.experimental import pallas as pl
from jax.experimental.pallas import tpu as pltpu
from jax.sharding import PartitionSpec as P

N = 256
ROWS, COLS = 32, 8
ZL, YL, XL = N // COLS, N // ROWS, N // ROWS
BANDS = 8
PIECE = 20
LANES = 128
f32 = jnp.float32
bf16 = jnp.bfloat16


@functools.cache
def tables():
    k = np.arange(N)
    angle = 2.0 * np.pi * ((k[:, None] * k[None, :]) % N) / N
    weight = 6.0 / ((4.0 + 2.0 * np.cos(2.0 * np.pi * k / N)) * np.sqrt(N))
    both = np.concatenate([np.cos(angle) * weight[None, :], np.sin(angle) * weight[None, :]])
    by_rest = both.reshape(2 * N, ROWS, YL).swapaxes(1, 2).reshape(2 * N, N)
    out = []
    for whole in (both, by_rest):
        high = whole.astype(ml_dtypes.bfloat16)
        low = (whole - high.astype(np.float64)).astype(ml_dtypes.bfloat16)
        out += [high, low]
    return tuple(out)


def split(value):
    high = value.astype(bf16)
    return high, (value - high.astype(f32)).astype(bf16)


def product(w_high, w_low, value, dims):
    high, low = split(value)

    def one(left, right):
        return lax.dot_general(left, right, (dims, ((), ())), preferred_element_type=f32)

    return one(w_high, high) + (one(w_high, low) + one(w_low, high))


def exchange_blocks(vs):
    lane = lax.broadcasted_iota(jnp.int32, (8, LANES), 1)
    low = lane < 64
    even = (lane & 32) == 0
    u = list(vs)
    for i in (0, 1):
        a, b = u[i], u[i + 2]
        u[i] = jnp.where(low, a, pltpu.roll(b, 64, 1))
        u[i + 2] = jnp.where(low, pltpu.roll(a, 64, 1), b)
    for i in (0, 2):
        a, b = u[i], u[i + 1]
        u[i] = jnp.where(even, a, pltpu.roll(b, 32, 1))
        u[i + 1] = jnp.where(even, pltpu.roll(a, 96, 1), b)
    return u


def pack(coef_ref, bands_ref, wh_hbm, wl_hbm, out_ref, cbuf, buf, wh_ref, wl_ref, spec, sems):
    halves = [pl.ds(h * LANES, LANES) for h in range(2)]
    starts = [pltpu.make_async_copy(coef_ref.at[:, halves[h]], cbuf.at[h], sems.at[h]) for h in range(2)]
    starts += [
        pltpu.make_async_copy(wh_hbm, wh_ref, sems.at[2 + 2 * BANDS]),
        pltpu.make_async_copy(wl_hbm, wl_ref, sems.at[3 + 2 * BANDS]),
    ]
    copies = [
        [pltpu.make_async_copy(bands_ref.at[b, :, halves[h]], buf.at[b, h], sems.at[2 + 2 * b + h]) for h in range(2)]
        for b in range(BANDS)
    ]
    for copy in starts + sum(copies, []):
        copy.start()
    def turn(b):
        for xh in range(2):
            for yh in range(2):
                block = jnp.concatenate([buf[b, xh, pl.ds(yh * 4 + k, ZL, stride=YL), :] for k in range(4)])
                turned = block.T
                for r in range(16):
                    row = b * ROWS * PIECE + PIECE * (xh * 16 + r) + 8 * yh
                    out_ref[pl.ds(row, 8), :] = turned[r * 8 : r * 8 + 8]

    def wait(bands):
        for b in bands:
            for copy in copies[b]:
                copy.wait()

    for step, bands in enumerate(STEPS):
        wait(bands)
        if step == DFT_AT:
            for copy in starts:
                copy.wait()
            rows = [
                jnp.concatenate([cbuf[h, pl.ds(part * N + y, ZL, stride=YL), :] for h in range(2)], axis=1)
                for part in range(2)
                for y in range(YL)
            ]
            q = product(wh_ref[...], wl_ref[...], jnp.concatenate(rows), ((1,), (1,)))
            for h in range(2):
                one, two = (slice(p * N + h * LANES, p * N + (h + 1) * LANES) for p in range(2))
                spec[h, pl.ds(0, N), :] = q[:N, one] - q[N:, two]
                spec[h, pl.ds(N, N), :] = q[N:, one] + q[:N, two]
        for b in bands:
            turn(b)
    for b in range(BANDS):
        for part in range(2):
            for yh in range(2):
                for g in range(ROWS // 8):
                    out_ref[pl.ds(b * ROWS * PIECE + PIECE * 8 * g + 16 + part * 2 + yh, 8, stride=PIECE), :] = spec[
                        yh, pl.ds(part * N + g * 64 + b, 8, stride=8), :
                    ]


EDGES = (0, 8, 16, 24, 32)
TRANSFORM_AT = 0
STEPS = ((0, 1, 2, 3), (4, 5, 6, 7))
DFT_AT = 0


def unpack(in_ref, yh_ref, yl_ref, wh_ref, wl_ref, coefs_ref, table_ref, cout, tab, field, sems):
    flat = tab.reshape(2, XL * (N + 8), LANES)
    copies = []

    def transform():
        for part in range(2):
            for yh in range(2):
                for g in range(ROWS // 8):
                    for h in range(2):
                        vs = [
                            in_ref[
                                pl.ds(PIECE * ((h * 4 + c) * ROWS + g * 8) + 16 + part * 2 + yh, 8, stride=PIECE), :
                            ]
                            for c in range(4)
                        ]
                        for k, v in enumerate(exchange_blocks(vs)):
                            field[pl.ds((yh * 4 + k) * ROWS + g * 8, 8), pl.ds(part * N + h * LANES, LANES)] = v
        q = product(yh_ref[...], yl_ref[...], field[...], ((1,), (0,)))
        along = jnp.concatenate([q[:N, :N] - q[N:, N:], q[N:, :N] + q[:N, N:]])
        q = product(wh_ref[...], wl_ref[...], along, ((1,), (1,)))
        real = q[:N, :N] - q[N:, N:]
        imag = q[N:, :N] + q[:N, N:]
        for h in range(2):
            lanes = slice(h * LANES, (h + 1) * LANES)
            cout[pl.ds(h, N, stride=2), :] = real[:, lanes]
            cout[pl.ds(2 * N + h, N, stride=2), :] = imag[:, lanes]
        copies.append(pltpu.make_async_copy(cout, coefs_ref, sems.at[2 * len(EDGES)]))
        copies[-1].start()

    for group, (first, last) in enumerate(zip(EDGES[:-1], EDGES[1:])):
        if group == TRANSFORM_AT:
            transform()
        for h in range(2):
            for r in range(first, last):
                for yh in range(2):
                    vs = [in_ref[pl.ds(PIECE * ((h * 4 + c) * ROWS + r) + 8 * yh, 8), :] for c in range(4)]
                    for k, v in enumerate(exchange_blocks(vs)):
                        flat[h, pl.ds(r * YL + yh * 4 + k, XL, stride=N + 8), :] = v
            where = pl.ds(first * YL, (last - first) * YL)
            copies.append(
                pltpu.make_async_copy(
                    tab.at[h, :, where, :],
                    table_ref.at[:, where, pl.ds(h * LANES, LANES)],
                    sems.at[2 * group + h],
                )
            )
            copies[-1].start()
    if TRANSFORM_AT == len(EDGES) - 1:
        transform()
    for copy in copies:
        copy.wait()


vmem = pl.BlockSpec(memory_space=pltpu.VMEM)
anywhere = pl.BlockSpec(memory_space=pltpu.HBM)


def local(coefficients, real_bands):
    assert coefficients.shape == (2, 1, ZL, YL, N)
    assert real_bands.shape == (BANDS, ZL, YL, N)
    assert (lax.axis_size("row"), lax.axis_size("col")) == (ROWS, COLS)
    wh, wl, yh, yl = (jnp.asarray(t) for t in tables())
    total = ROWS * COLS * PIECE
    packed = pl.pallas_call(
        pack,
        name="pack",
        out_shape=jax.ShapeDtypeStruct((total, LANES), f32),
        in_specs=[anywhere] * 4,
        out_specs=vmem,
        scratch_shapes=[
            pltpu.VMEM((2, 2 * ZL * YL, LANES), f32),
            pltpu.VMEM((BANDS, 2, ZL * YL, LANES), f32),
            pltpu.VMEM((2 * N, N), bf16),
            pltpu.VMEM((2 * N, N), bf16),
            pltpu.VMEM((2, 2 * N, LANES), f32),
            pltpu.SemaphoreType.DMA((4 + 2 * BANDS,)),
        ],
        compiler_params=pltpu.CompilerParams(vmem_limit_bytes=24 << 20),
    )(
        pltpu.with_memory_space_constraint(coefficients.reshape(2 * ZL * YL, N), pltpu.HBM),
        pltpu.with_memory_space_constraint(real_bands.reshape(BANDS, ZL * YL, N), pltpu.HBM),
        pltpu.with_memory_space_constraint(wh, pltpu.HBM),
        pltpu.with_memory_space_constraint(wl, pltpu.HBM),
    )
    packed = packed.reshape(ROWS * COLS, PIECE // 4, 4, LANES)
    got = lax.all_to_all(packed, ("col", "row"), split_axis=0, concat_axis=0, tiled=True)
    coefs, table = pl.pallas_call(
        unpack,
        name="unpack",
        out_shape=[
            jax.ShapeDtypeStruct((4 * N, LANES), f32),
            jax.ShapeDtypeStruct((XL, N, N), f32),
        ],
        in_specs=[vmem] * 5,
        out_specs=[anywhere, anywhere],
        scratch_shapes=[
            pltpu.VMEM((4 * N, LANES), f32),
            pltpu.VMEM((2, XL, N + 8, LANES), f32),
            pltpu.VMEM((N, 2 * N), f32),
            pltpu.SemaphoreType.DMA((2 * len(EDGES) + 1,)),
        ],
        compiler_params=pltpu.CompilerParams(vmem_limit_bytes=24 << 20),
    )(got.reshape(total, LANES), yh, yl, wh, wl)
    return coefs.reshape(2, 1, N, 1, N), table.reshape(1, XL, N, N)


def solution(mesh):
    placed = (P(None, None, "col", "row", None), P(None, "col", "row", None))
    return jax.shard_map(
        local,
        mesh=mesh,
        in_specs=placed,
        out_specs=(P(None, None, None, ("row", "col"), None), P("col", "row", None, None)),
        check_vma=False,
    )
```

time: 91.7 us -> 86.3 us (0.941)
  local copies, waits for them, and re-layouts: 4.55 us -> 0.03 us
    unnamed x16 -> x8, local copies, waits for them, and re-layouts: 4.55 us -> 0.03 us
where the time goes in v2:
time: 86.3 us; the launch traced here: 86.1 us
  blocking collectives  78.3 us (91%)
  Pallas kernels  7.07 us (8%)
    all_to_all x1, blocking collectives, local(): lax.all_to_all(packed, ('col', 'row'), split_axis=0, concat_axis=0, tiled...  78.3 us
    pallas_call x1, Pallas kernels, local(): pl.pallas_call(unpack, name='unpack', out_shape=[jax.ShapeDtypeStruct((4...  4.29 us
    pallas_call x1, Pallas kernels, local(): pl.pallas_call(pack, name='pack', out_shape=jax.ShapeDtypeStruct((total,...  2.78 us

profile of v2, /device:TPU:8, one launch (start us, length us, event | category | flops | bytes accessed | tf_op | source)
XLA Modules:
  0.0 86.1 jit_solution(127484574725026377)
XLA Ops:
  0.6 2.8 %pack.1 = f32[5120,128]{1,0:T(8,128)S(1)} custom-call(f32[512,256]{1,0:T(8,128)} %bitcast.9, f32[8,256,256]{2,1,0:T(8,128)} %bitcast.8, bf16[512,256]{1,0:T(8,128)(2,1)} %constant.8.clone.wh_hbm.wh_ref, bf16[512,256]{1,0:T(8,128)(2,1)} %constant.9.clone.wl_hbm.wl_ref), custom_call_target="tpu_custom_call" | custom-call | tf_op jit(solution)/shard_map/pack/pallas_call | solution.py:189
  3.4 0.0 copy-start
  3.4 0.0 copy-start.1
  3.4 0.0 copy-start.2
  3.5 0.0 copy-start.3
  3.5 78.3 %all_to_all.5 = f32[256,5,4,128]{3,2,1,0:T(4,128)S(1)} all-to-all(f32[256,5,4,128]{3,2,1,0:T(4,128)S(1)} %bitcast.7), channel_id=1, replica_groups=mesh['row'=32,'col'=8] {'col','row'}, dimensions={0} | all-to-all | bytes 5242880 | tf_op jit(solution)/shard_map/all_to_all | solution.py:211
  81.8 0.0 copy-done
  81.8 0.0 copy-done.1
  81.8 0.0 copy-done.2
  81.8 0.0 copy-done.3
  81.8 4.3 %unpack.1 = (f32[1024,128]{1,0:T(8,128)}, f32[8,256,256]{2,1,0:T(8,128)}) custom-call(f32[5120,128]{1,0:T(8,128)S(1)} %bitcast.6, bf16[512,256]{1,0:T(8,128)(2,1)S(1)} %copy-done.3, bf16[512,256]{1,0:T(8,128)(2,1)S(1)} %copy-done.2, bf16[512,256]{1,0:T(8,128)(2,1)S(1)} %copy-done.1, bf16[512,256]{1,0:T(8,128)(2,1)S(1)} %copy-done), custom_call_target="tpu_custom_call" | custom-call | tf_op jit(solution)/shard_map/unpack/pallas_call | solution.py:212
Async XLA Ops:
  3.4 78.4 %copy-start = (bf16[512,256]{1,0:T(8,128)(2,1)S(1)}, bf16[512,256]{1,0:T(8,128)(2,1)}, u32[]{:S(2)}) copy-start(bf16[512,256]{1,0:T(8,128)(2,1)} %constant.9.clone.wl_hbm.wl_ref) | copy-start | bytes 786436
  3.4 78.4 %copy-start.1 = (bf16[512,256]{1,0:T(8,128)(2,1)S(1)}, bf16[512,256]{1,0:T(8,128)(2,1)}, u32[]{:S(2)}) copy-start(bf16[512,256]{1,0:T(8,128)(2,1)} %constant.8.clone.wh_hbm.wh_ref) | copy-start | bytes 786436
  3.4 78.4 %copy-start.2 = (bf16[512,256]{1,0:T(8,128)(2,1)S(1)}, bf16[512,256]{1,0:T(8,128)(2,1)}, u32[]{:S(2)}) copy-start(bf16[512,256]{1,0:T(8,128)(2,1)} %constant.11.clone.yl_ref) | copy-start | bytes 786436
  3.5 78.4 %copy-start.3 = (bf16[512,256]{1,0:T(8,128)(2,1)S(1)}, bf16[512,256]{1,0:T(8,128)(2,1)}, u32[]{:S(2)}) copy-start(bf16[512,256]{1,0:T(8,128)(2,1)} %constant.10.clone.yh_ref) | copy-start | bytes 786436

commit v3 on v2

v3 whole, which is shorter than its diff:
```python
import functools

import jax
import jax.numpy as jnp
import ml_dtypes
import numpy as np
from jax import lax
from jax.experimental import pallas as pl
from jax.experimental.pallas import tpu as pltpu
from jax.sharding import PartitionSpec as P

N = 256
ROWS, COLS = 32, 8
ZL, YL, XL = N // COLS, N // ROWS, N // ROWS
BANDS = 8
ZD, PLANE = 8, 32
PIECE = 10 * PLANE
SLOT = 10 * ZD
LANES = 128
f32 = jnp.float32
bf16 = jnp.bfloat16


@functools.cache
def tables():
    k = np.arange(N)
    angle = 2.0 * np.pi * ((k[:, None] * k[None, :]) % N) / N
    weight = 6.0 / ((4.0 + 2.0 * np.cos(2.0 * np.pi * k / N)) * np.sqrt(N))
    both = np.concatenate([np.cos(angle) * weight[None, :], np.sin(angle) * weight[None, :]])
    by_rest = both.reshape(2 * N, ZD, ROWS // ZD, YL).swapaxes(1, 2).reshape(2 * N, N)
    out = []
    for whole in (both, by_rest):
        high = whole.astype(ml_dtypes.bfloat16)
        low = (whole - high.astype(np.float64)).astype(ml_dtypes.bfloat16)
        out += [high, low]
    return tuple(out)


def split(value):
    high = value.astype(bf16)
    return high, (value - high.astype(f32)).astype(bf16)


def product(w_high, w_low, value, dims):
    high, low = split(value)

    def one(left, right):
        return lax.dot_general(left, right, (dims, ((), ())), preferred_element_type=f32)

    return one(w_high, high) + (one(w_high, low) + one(w_low, high))


def exchange_blocks(vs):
    lane = lax.broadcasted_iota(jnp.int32, vs[0].shape, 1)
    low = lane < 64
    even = (lane & 32) == 0
    out = []
    for q in range(4):
        a, b, c, d = (vs[(place - q) % 4] for place in range(4))
        u = jnp.where(low, jnp.where(even, a, b), jnp.where(even, c, d))
        out.append(pltpu.roll(u, LANES - 32 * q, 1) if q else u)
    return out


def pack(coef_ref, bands_ref, wh_hbm, wl_hbm, one_ref, two_ref, cbuf, buf, wh_ref, wl_ref, spec, sems):
    halves = [pl.ds(h * LANES, LANES) for h in range(2)]
    mine = lax.axis_index("y")
    turn_by = [lax.rem(k + 4 - mine, 4) for k in range(4)]
    hops = [lax.rem(z + ZD - lax.axis_index("z"), ZD) for z in range(ZD)]
    starts = [pltpu.make_async_copy(coef_ref.at[:, halves[h]], cbuf.at[h], sems.at[h]) for h in range(2)]
    starts += [
        pltpu.make_async_copy(wh_hbm, wh_ref, sems.at[2 + 2 * BANDS]),
        pltpu.make_async_copy(wl_hbm, wl_ref, sems.at[3 + 2 * BANDS]),
    ]
    copies = [
        [pltpu.make_async_copy(bands_ref.at[b, :, halves[h]], buf.at[b, h], sems.at[2 + 2 * b + h]) for h in range(2)]
        for b in range(BANDS)
    ]
    for copy in starts + sum(copies, []):
        copy.start()

    def turn(b):
        for xh in range(2):
            for yh in range(2):
                block = jnp.concatenate(
                    [buf[b, xh, pl.ds(yh * 4 + turn_by[k], ZL, stride=YL), :] for k in range(4)]
                )
                turned = block.T
                for r in range(16):
                    hop, place = hops[xh * 4 + r // 4], r % 4 * COLS + b
                    value = turned[r * 8 : r * 8 + 8]
                    if yh == 0:
                        one_ref[pl.ds(pl.multiple_of(hop * PIECE + place * 8, 8), 8), :] = value
                    else:
                        two_ref[pl.ds(pl.multiple_of(place * SLOT + hop * 8, 8), 8), :] = value

    for step, bands in enumerate(STEPS):
        for b in bands:
            for copy in copies[b]:
                copy.wait()
        if step == DFT_AT:
            for copy in starts:
                copy.wait()
            rows = [
                jnp.concatenate(
                    [cbuf[h, pl.ds(part * N + y // 4 * 4 + turn_by[y % 4], ZL, stride=YL), :] for h in range(2)],
                    axis=1,
                )
                for part in range(2)
                for y in range(YL)
            ]
            q = product(wh_ref[...], wl_ref[...], jnp.concatenate(rows), ((1,), (1,)))
            for h in range(2):
                one, two = (slice(p * N + h * LANES, p * N + (h + 1) * LANES) for p in range(2))
                spec[h, pl.ds(0, N), :] = q[:N, one] - q[N:, two]
                spec[h, pl.ds(N, N), :] = q[N:, one] + q[:N, two]
        for b in bands:
            turn(b)
    for b in range(BANDS):
        for yh in range(2):
            for z in range(ZD):
                for part in range(2):
                    value = spec[yh, pl.ds(part * N + z * 32 + b, 4, stride=8), :]
                    if part == 0:
                        one_ref[pl.ds(hops[z] * PIECE + 8 * PLANE + yh * PLANE + b, 4, stride=COLS), :] = value
                    else:
                        two_ref[pl.ds(b * SLOT + 8 * ZD + hops[z] * 2 + yh, 4, stride=COLS * SLOT), :] = value


STEPS = ((0, 1, 2, 3), (4, 5, 6, 7))
DFT_AT = 0


def regroup(in_ref, *out_refs):
    for k, out_ref in enumerate(out_refs):
        for p in range(PLANE):
            out_ref[pl.ds(p * 8, 8), :] = in_ref[pl.ds(p * SLOT + k * 8, 8), :]
        for j in range(2):
            for g in range(PLANE // 8):
                out_ref[pl.ds(PLANE * 8 + j * PLANE + g * 8, 8), :] = in_ref[
                    pl.ds(g * 8 * SLOT + 8 * ZD + k * 2 + j, 8, stride=SLOT), :
                ]


def join(*refs):
    *in_refs, out_ref = refs
    for k, in_ref in enumerate(in_refs):
        for p in range(PLANE):
            out_ref[pl.ds(p * SLOT + k * 8, 8), :] = in_ref[pl.ds(p * 8, 8), :]
        for j in range(2):
            for g in range(PLANE // 8):
                out_ref[pl.ds(g * 8 * SLOT + 8 * ZD + k * 2 + j, 8, stride=SLOT), :] = in_ref[
                    pl.ds(PLANE * 8 + j * PLANE + g * 8, 8), :
                ]


def unpack(*refs):
    one_ref, *two_refs = refs[: ZD + 1]
    tables_hbm, (coefs_ref, table_ref, *held, cout, tab, field, sems) = refs[ZD + 1 : ZD + 5], refs[ZD + 5 :]
    yh_ref, yl_ref, wh_ref, wl_ref = held
    fetches = [
        pltpu.make_async_copy(source, target, sems.at[2 * ZD + 1 + i])
        for i, (source, target) in enumerate(zip(tables_hbm, held))
    ]
    for fetch in fetches:
        fetch.start()
    flat = tab.reshape(2, XL * (N + 8), LANES)
    source = [lax.rem(lax.axis_index("z") + ZD - k, ZD) for k in range(ZD)]
    for k in range(ZD):
        for part in range(2):
            for yh in range(2):
                for h in range(2):
                    if part == 0:
                        first = h * 4 * SLOT + 8 * ZD + k * 2 + yh
                        vs = [one_ref[pl.ds(first + c * SLOT, 4, stride=COLS * SLOT), :] for c in range(4)]
                    else:
                        first = PLANE * 8 + yh * PLANE + h * 4
                        vs = [two_refs[k][pl.ds(first + c, 4, stride=COLS), :] for c in range(4)]
                    for y, v in enumerate(exchange_blocks(vs)):
                        field[h, pl.ds(part * N + source[k] * 8 + yh * 4 + y, 4, stride=64), :] = v
    for fetch in fetches:
        fetch.wait()
    values = jnp.concatenate([field[0], field[1]], axis=1)
    q = product(yh_ref[...], yl_ref[...], jnp.concatenate([values[:N], values[N:]], axis=1), ((1,), (0,)))
    along = jnp.concatenate([q[:N, :N] - q[N:, N:], q[N:, :N] + q[:N, N:]])
    q = product(wh_ref[...], wl_ref[...], along, ((1,), (1,)))
    real = q[:N, :N] - q[N:, N:]
    imag = q[N:, :N] + q[:N, N:]
    for h in range(2):
        lanes = slice(h * LANES, (h + 1) * LANES)
        cout[pl.ds(h, N, stride=2), :] = real[:, lanes]
        cout[pl.ds(2 * N + h, N, stride=2), :] = imag[:, lanes]
    copies = [pltpu.make_async_copy(cout, coefs_ref, sems.at[2 * ZD])]
    copies[0].start()
    for k in range(ZD):
        for h in range(2):
            for r in range(4):
                for yh in range(2):
                    places = [r * COLS + h * 4 + c for c in range(4)]
                    if yh == 0:
                        vs = [one_ref[pl.ds(p * SLOT + k * 8, 8), :] for p in places]
                    else:
                        vs = [two_refs[k][pl.ds(p * 8, 8), :] for p in places]
                    for y, v in enumerate(exchange_blocks(vs)):
                        flat[h, pl.ds(source[k] * 32 + r * 8 + yh * 4 + y, XL, stride=N + 8), :] = v
            where = pl.ds(pl.multiple_of(source[k] * 32, 32), 32)
            copies.append(
                pltpu.make_async_copy(
                    tab.at[h, :, where, :], table_ref.at[:, where, pl.ds(h * LANES, LANES)], sems.at[2 * k + h]
                )
            )
            copies[-1].start()
    for copy in copies:
        copy.wait()


vmem = pl.BlockSpec(memory_space=pltpu.VMEM)
anywhere = pl.BlockSpec(memory_space=pltpu.HBM)
plane = ("xh", "core", "xl", "y")


def by_hop(values):
    shift = [[(z, (z + k) % ZD) for z in range(ZD)] for k in range(ZD)]
    out = [values[0]] + [None] * (ZD - 1)
    for k in HOPS:
        out[k] = lax.ppermute(values[k], "z", shift[k])
    return out


HOPS = (3, 5, 4, 2, 6, 1, 7)


def local(coefficients, real_bands):
    assert coefficients.shape == (2, 1, ZL, YL, N)
    assert real_bands.shape == (BANDS, ZL, YL, N)
    wh, wl, yh, yl = (jnp.asarray(t) for t in tables())
    params = pltpu.CompilerParams(vmem_limit_bytes=16 << 20)
    one, two = pl.pallas_call(
        pack,
        name="pack",
        out_shape=[
            jax.ShapeDtypeStruct((ZD * PIECE, LANES), f32),
            jax.ShapeDtypeStruct((PLANE * SLOT, LANES), f32),
        ],
        in_specs=[anywhere] * 4,
        out_specs=[vmem, vmem],
        scratch_shapes=[
            pltpu.VMEM((2, 2 * ZL * YL, LANES), f32),
            pltpu.VMEM((BANDS, 2, ZL * YL, LANES), f32),
            pltpu.VMEM((2 * N, N), bf16),
            pltpu.VMEM((2 * N, N), bf16),
            pltpu.VMEM((2, 2 * N, LANES), f32),
            pltpu.SemaphoreType.DMA((4 + 2 * BANDS,)),
        ],
        compiler_params=params,
    )(
        pltpu.with_memory_space_constraint(coefficients.reshape(2 * ZL * YL, N), pltpu.HBM),
        pltpu.with_memory_space_constraint(real_bands.reshape(BANDS, ZL * YL, N), pltpu.HBM),
        pltpu.with_memory_space_constraint(wh, pltpu.HBM),
        pltpu.with_memory_space_constraint(wl, pltpu.HBM),
    )
    two = lax.all_to_all(two.reshape(PLANE, SLOT, LANES), plane, split_axis=0, concat_axis=0, tiled=True)
    one = one.reshape(ZD, PIECE, LANES)
    one = by_hop([one[k] for k in range(ZD)])
    parts = pl.pallas_call(
        regroup,
        name="regroup",
        out_shape=[jax.ShapeDtypeStruct((PIECE, LANES), f32)] * ZD,
        in_specs=[vmem],
        out_specs=[vmem] * ZD,
        compiler_params=params,
    )(two.reshape(PLANE * SLOT, LANES))
    parts = by_hop(parts)
    one = pl.pallas_call(
        join,
        name="join",
        out_shape=jax.ShapeDtypeStruct((ZD * PIECE, LANES), f32),
        in_specs=[vmem] * ZD,
        out_specs=vmem,
        compiler_params=params,
    )(*one)
    one = one.reshape(PLANE, SLOT, LANES)
    one = lax.all_to_all(one, plane, split_axis=0, concat_axis=0, tiled=True)
    coefs, table = pl.pallas_call(
        unpack,
        name="unpack",
        out_shape=[
            jax.ShapeDtypeStruct((4 * N, LANES), f32),
            jax.ShapeDtypeStruct((XL, N, N), f32),
        ],
        in_specs=[vmem] * (ZD + 1) + [anywhere] * 4,
        out_specs=[anywhere, anywhere],
        scratch_shapes=[
            *[pltpu.VMEM((2 * N, N), bf16)] * 4,
            pltpu.VMEM((4 * N, LANES), f32),
            pltpu.VMEM((2, XL, N + 8, LANES), f32),
            pltpu.VMEM((2, 2 * N, LANES), f32),
            pltpu.SemaphoreType.DMA((2 * ZD + 5,)),
        ],
        compiler_params=params,
    )(
        one.reshape(PLANE * SLOT, LANES),
        *parts,
        *[pltpu.with_memory_space_constraint(t, pltpu.HBM) for t in (yh, yl, wh, wl)],
    )
    return coefs.reshape(2, 1, N, 1, N), table.reshape(1, XL, N, N)


def solution(mesh):
    split = jax.sharding.Mesh(mesh.devices.reshape(ZD, 2, 2, 2, 4), ("z", "xh", "core", "xl", "y"))
    row, col = ("z", "xh", "core"), ("xl", "y")
    return jax.shard_map(
        local,
        mesh=split,
        in_specs=(P(None, None, col, row, None), P(None, col, row, None)),
        out_specs=(P(None, None, None, row + col, None), P(col, row, None, None)),
        check_vma=False,
    )
```

time: 86.3 us -> 107 us (1.24); the launches traced: 86.1 us -> 106 us
  blocking collectives: 78.3 us -> 0 us
  waiting for transfers between devices: 0 us -> 53.6 us
  starting transfers between devices: 0 us -> 40 us
  Pallas kernels: 7.07 us -> 10 us
  local copies, waits for them, and re-layouts: 0.03 us -> 1.16 us
    all_to_all x1 -> x0, blocking collectives: 78.3 us -> none  [local(): lax.all_to_all(packed, ('col', 'row'), split_axis=0, concat_axis=0, tiled...]
    ppermute x0 -> x14, waiting for transfers between devices: none -> 53.6 us  [by_hop(): out[k] = lax.ppermute(values[k], 'z', shift[k])]
    ppermute x0 -> x14, starting transfers between devices: none -> 25.1 us  [by_hop(): out[k] = lax.ppermute(values[k], 'z', shift[k])]
    all_to_all x0 -> x2, starting transfers between devices: none -> 15 us  [the longest x1 7.54 us: local(): lax.all_to_all(two.reshape(PLANE, SLOT, LANES), plane, split_axis=0, conc...]
    pallas_call x1 -> x3, Pallas kernels: 2.78 us -> 4.32 us  [the longest x1 3.98 us: local(): pl.pallas_call(pack, name='pack', out_shape=[jax.ShapeDtypeStruct((ZD * P...]
    pallas_call x1, Pallas kernels: 4.29 us -> 5.7 us  [local(): pl.pallas_call(unpack, name='unpack', out_shape=[jax.ShapeDtypeStruct((4...]
  transfers between devices with their start and end apart: 0 -> 16, of which waited for: 0 -> 11; matrix products, arithmetic and copies ran while one was open for 0% -> 0% of each run, Pallas kernels for 0% -> 0%
where the time goes in v3:
time: 107 us; the launch traced here: 106 us
  waiting for transfers between devices  53.6 us (50%)
  starting transfers between devices  40 us (37%)
  Pallas kernels  10 us (9%)
  local copies, waits for them, and re-layouts  1.16 us (1%)
    ppermute x14, waiting for transfers between devices, by_hop(): out[k] = lax.ppermute(values[k], 'z', shift[k])  53.6 us
    ppermute x14, starting transfers between devices, by_hop(): out[k] = lax.ppermute(values[k], 'z', shift[k])  25.1 us
    all_to_all x1, starting transfers between devices, local(): lax.all_to_all(two.reshape(PLANE, SLOT, LANES), plane, split_axis=0, conc...  7.54 us
    all_to_all x1, starting transfers between devices, local(): one = lax.all_to_all(one, plane, split_axis=0, concat_axis=0, tiled=True)  7.42 us
    pallas_call x1, Pallas kernels, local(): pl.pallas_call(unpack, name='unpack', out_shape=[jax.ShapeDtypeStruct((4...  5.7 us
    pallas_call x1, Pallas kernels, local(): pl.pallas_call(pack, name='pack', out_shape=[jax.ShapeDtypeStruct((ZD * P...  3.98 us
  transfers between devices with their start and end apart: 16, of which 11 were waited for; matrix products, arithmetic and copies ran while one was open for 0% of the time, Pallas kernels for 0%

profile of v3, /device:TPU:8, one launch (start us, length us, event | category | flops | bytes accessed | tf_op | source)
XLA Modules:
  0.0 105.6 jit_solution(12911948474298679294)
XLA Ops:
  0.6 4.0 %pack.1 = (f32[2560,128]{1,0:T(8,128)S(1)}, f32[2560,128]{1,0:T(8,128)}) custom-call(f32[512,256]{1,0:T(8,128)} %bitcast.12, f32[8,256,256]{2,1,0:T(8,128)} %bitcast.11, bf16[512,256]{1,0:T(8,128)(2,1)} %constant.8.clone.wh_hbm.refs_11_, bf16[512,256]{1,0:T(8,128)(2,1)} %constant.9.clone.wl_hbm.refs_12_), custom_call_target="tpu_custom_call" | custom-call | tf_op jit(solution)/shard_map/pack/pallas_call | solution.py:238
  4.6 7.5 %all-to-all-start.1 = ((f32[32,80,128]{2,1,0:T(8,128)}), f32[32,80,128]{2,1,0:T(8,128)S(1)}, u32[]{:S(2)}, u32[]{:S(2)}) async-start(f32[32,80,128]{2,1,0:T(8,128)} %bitcast.4), calls=%async_computation.1 | async-start | bytes 2621440 | tf_op jit(solution)/shard_map/all_to_all | solution.py:262
  12.2 0.1 fusion
  12.3 5.9 %collective-permute-start.6 = (f32[320,128]{1,0:T(8,128)S(1)}, f32[320,128]{1,0:T(8,128)S(1)}, u32[]{:S(2)}, u32[]{:S(2)}) collective-permute-start(f32[320,128]{1,0:T(8,128)S(1)} %get-tuple-element.28), channel_id=1, source_target_pairs={{0,224},{32,0},{64,32},{96,64},{128,96},{160,128},{192,160},{224,1... | collective-permute-start | bytes 491528 | tf_op jit(solution)/shard_map/ppermute | solution.py:226
  18.2 1.4 %collective-permute-start.5 = (f32[320,128]{1,0:T(8,128)S(1)}, f32[320,128]{1,0:T(8,128)S(1)}, u32[]{:S(2)}, u32[]{:S(2)}) collective-permute-start(f32[320,128]{1,0:T(8,128)S(1)} %get-tuple-element.29), channel_id=1, source_target_pairs={{0,192},{32,224},{64,0},{96,32},{128,64},{160,96},{192,128},{224,1... | collective-permute-start | bytes 491528 | tf_op jit(solution)/shard_map/ppermute | solution.py:226
  19.7 0.4 collective-permute-start.4
  20.1 5.0 %collective-permute-start.3 = (f32[320,128]{1,0:T(8,128)S(1)}, f32[320,128]{1,0:T(8,128)S(1)}, u32[]{:S(2)}, u32[]{:S(2)}) collective-permute-start(f32[320,128]{1,0:T(8,128)S(1)} %get-tuple-element.31), channel_id=1, source_target_pairs={{0,128},{32,160},{64,192},{96,224},{128,0},{160,32},{192,64},{224,... | collective-permute-start | bytes 491528 | tf_op jit(solution)/shard_map/ppermute | solution.py:226
  25.1 0.0 collective-permute-start.2
  25.1 0.7 collective-permute-done.6.refs_7_
  25.8 1.8 %collective-permute-start.1 = (f32[320,128]{1,0:T(8,128)S(1)}, f32[320,128]{1,0:T(8,128)S(1)}, u32[]{:S(2)}, u32[]{:S(2)}) collective-permute-start(f32[320,128]{1,0:T(8,128)S(1)} %get-tuple-element.33), channel_id=1, source_target_pairs={{0,64},{32,96},{64,128},{96,160},{128,192},{160,224},{192,0},{224,... | collective-permute-start | bytes 491528 | tf_op jit(solution)/shard_map/ppermute | solution.py:226
  27.6 4.8 %collective-permute-done.5.refs_6_ = f32[320,128]{1,0:T(8,128)S(1)} collective-permute-done((f32[320,128]{1,0:T(8,128)S(1)}, f32[320,128]{1,0:T(8,128)S(1)}, u32[]{:S(2)}, u32[]{:S(2)}) %collective-permute-start.5) | collective-permute-done | bytes 163872 | tf_op jit(solution)/shard_map/ppermute | solution.py:226
  32.4 0.0 collective-permute-start
  32.4 14.1 %collective-permute-done.4.refs_5_ = f32[320,128]{1,0:T(8,128)S(1)} collective-permute-done((f32[320,128]{1,0:T(8,128)S(1)}, f32[320,128]{1,0:T(8,128)S(1)}, u32[]{:S(2)}, u32[]{:S(2)}) %collective-permute-start.4) | collective-permute-done | bytes 163872 | tf_op jit(solution)/shard_map/ppermute | solution.py:226
  46.5 0.0 collective-permute-done.3.refs_4_
  46.5 1.2 %collective-permute-done.2.refs_3_ = f32[320,128]{1,0:T(8,128)S(1)} collective-permute-done((f32[320,128]{1,0:T(8,128)S(1)}, f32[320,128]{1,0:T(8,128)S(1)}, u32[]{:S(2)}, u32[]{:S(2)}) %collective-permute-start.2) | collective-permute-done | bytes 163872 | tf_op jit(solution)/shard_map/ppermute | solution.py:226
  47.8 4.1 %collective-permute-done.1.refs_2_ = f32[320,128]{1,0:T(8,128)S(1)} collective-permute-done((f32[320,128]{1,0:T(8,128)S(1)}, f32[320,128]{1,0:T(8,128)S(1)}, u32[]{:S(2)}, u32[]{:S(2)}) %collective-permute-start.1) | collective-permute-done | bytes 163872 | tf_op jit(solution)/shard_map/ppermute | solution.py:226
  51.9 2.3 %collective-permute-done.refs_1_ = f32[320,128]{1,0:T(8,128)S(1)} collective-permute-done((f32[320,128]{1,0:T(8,128)S(1)}, f32[320,128]{1,0:T(8,128)S(1)}, u32[]{:S(2)}, u32[]{:S(2)}) %collective-permute-start) | collective-permute-done | bytes 163872 | tf_op jit(solution)/shard_map/ppermute | solution.py:226
  54.1 0.2 join.1
  54.3 0.0 copy-start
  54.3 1.1 %copy-done = f32[2560,128]{1,0:T(8,128)} copy-done((f32[2560,128]{1,0:T(8,128)}, f32[2560,128]{1,0:T(8,128)S(1)}, u32[]{:S(2)}) %copy-start) | copy-done | bytes 1310744
  55.4 0.0 all-to-all-done.1
  55.4 7.4 %all-to-all-start = ((f32[32,80,128]{2,1,0:T(8,128)}), f32[32,80,128]{2,1,0:T(8,128)S(1)}, u32[]{:S(2)}, u32[]{:S(2)}) async-start(f32[32,80,128]{2,1,0:T(8,128)} %bitcast.10), calls=%async_computation | async-start | bytes 2621440 | tf_op jit(solution)/shard_map/all_to_all | solution.py:283
  62.8 0.1 regroup.1
  63.0 1.1 %collective-permute-start.7 = (f32[320,128]{1,0:T(8,128)S(1)}, f32[320,128]{1,0:T(8,128)S(1)}, u32[]{:S(2)}, u32[]{:S(2)}) collective-permute-start(f32[320,128]{1,0:T(8,128)S(1)} %get-tuple-element.17), channel_id=1, source_target_pairs={{0,32},{32,64},{64,96},{96,128},{128,160},{160,192},{192,224},{224... | collective-permute-start | bytes 491528 | tf_op jit(solution)/shard_map/ppermute | solution.py:226
  64.1 1.0 collective-permute-start.8
  65.1 1.6 %collective-permute-start.9 = (f32[320,128]{1,0:T(8,128)S(1)}, f32[320,128]{1,0:T(8,128)S(1)}, u32[]{:S(2)}, u32[]{:S(2)}) collective-permute-start(f32[320,128]{1,0:T(8,128)S(1)} %get-tuple-element.19), channel_id=1, source_target_pairs={{0,96},{32,128},{64,160},{96,192},{128,224},{160,0},{192,32},{224,... | collective-permute-start | bytes 491528 | tf_op jit(solution)/shard_map/ppermute | solution.py:226
  66.7 4.8 %collective-permute-start.10 = (f32[320,128]{1,0:T(8,128)S(1)}, f32[320,128]{1,0:T(8,128)S(1)}, u32[]{:S(2)}, u32[]{:S(2)}) collective-permute-start(f32[320,128]{1,0:T(8,128)S(1)} %get-tuple-element.20), channel_id=1, source_target_pairs={{0,128},{32,160},{64,192},{96,224},{128,0},{160,32},{192,64},{224,... | collective-permute-start | bytes 491528 | tf_op jit(solution)/shard_map/ppermute | solution.py:226
  71.5 1.4 %collective-permute-start.11 = (f32[320,128]{1,0:T(8,128)S(1)}, f32[320,128]{1,0:T(8,128)S(1)}, u32[]{:S(2)}, u32[]{:S(2)}) collective-permute-start(f32[320,128]{1,0:T(8,128)S(1)} %get-tuple-element.21), channel_id=1, source_target_pairs={{0,160},{32,192},{64,224},{96,0},{128,32},{160,64},{192,96},{224,1... | collective-permute-start | bytes 491528 | tf_op jit(solution)/shard_map/ppermute | solution.py:226
  73.0 1.0 collective-permute-done.7.refs_2_
  73.9 0.5 collective-permute-start.12
  74.4 6.4 %collective-permute-done.8.refs_3_ = f32[320,128]{1,0:T(8,128)S(1)} collective-permute-done((f32[320,128]{1,0:T(8,128)S(1)}, f32[320,128]{1,0:T(8,128)S(1)}, u32[]{:S(2)}, u32[]{:S(2)}) %collective-permute-start.8) | collective-permute-done | bytes 163872 | tf_op jit(solution)/shard_map/ppermute | solution.py:226
  80.8 0.0 collective-permute-start.13
  80.8 10.2 %collective-permute-done.9.refs_4_ = f32[320,128]{1,0:T(8,128)S(1)} collective-permute-done((f32[320,128]{1,0:T(8,128)S(1)}, f32[320,128]{1,0:T(8,128)S(1)}, u32[]{:S(2)}, u32[]{:S(2)}) %collective-permute-start.9) | collective-permute-done | bytes 163872 | tf_op jit(solution)/shard_map/ppermute | solution.py:226
  91.0 0.0 collective-permute-done.10.refs_5_
  91.0 0.0 collective-permute-done.11.refs_6_
  91.0 5.4 %collective-permute-done.12.refs_7_ = f32[320,128]{1,0:T(8,128)S(1)} collective-permute-done((f32[320,128]{1,0:T(8,128)S(1)}, f32[320,128]{1,0:T(8,128)S(1)}, u32[]{:S(2)}, u32[]{:S(2)}) %collective-permute-start.12) | collective-permute-done | bytes 163872 | tf_op jit(solution)/shard_map/ppermute | solution.py:226
  96.4 3.4 %collective-permute-done.13.refs_8_ = f32[320,128]{1,0:T(8,128)S(1)} collective-permute-done((f32[320,128]{1,0:T(8,128)S(1)}, f32[320,128]{1,0:T(8,128)S(1)}, u32[]{:S(2)}, u32[]{:S(2)}) %collective-permute-start.13) | collective-permute-done | bytes 163872 | tf_op jit(solution)/shard_map/ppermute | solution.py:226
  99.8 0.0 all-to-all-done
  99.8 5.7 %unpack.1 = (f32[1024,128]{1,0:T(8,128)}, f32[8,256,256]{2,1,0:T(8,128)}) custom-call(f32[2560,128]{1,0:T(8,128)S(1)} %bitcast.8, f32[320,128]{1,0:T(8,128)S(1)} %get-tuple-element.16.refs_1_, f32[320,128]{1,0:T(8,128)S(1)} %collective-permute-done.7.refs_2_, f32[320,128]{1,0:T(8,128)S(1)} %collective-permute-done.8.refs_3_, ...), custom_call_target="tpu_custom_call" | custom-call | tf_op jit(solution)/shard_map/unpack/pallas_call | solution.py:284
Async XLA Ops:
  4.6 50.8 %all-to-all-start.1 = ((f32[32,80,128]{2,1,0:T(8,128)}), f32[32,80,128]{2,1,0:T(8,128)S(1)}, u32[]{:S(2)}, u32[]{:S(2)}) async-start(f32[32,80,128]{2,1,0:T(8,128)} %bitcast.4), calls=%async_computation.1 | async-start | bytes 2621440 | tf_op jit(solution)/shard_map/all_to_all | solution.py:262
  12.3 13.6 %collective-permute-start.6 = (f32[320,128]{1,0:T(8,128)S(1)}, f32[320,128]{1,0:T(8,128)S(1)}, u32[]{:S(2)}, u32[]{:S(2)}) collective-permute-start(f32[320,128]{1,0:T(8,128)S(1)} %get-tuple-element.28), channel_id=1, source_target_pairs={{0,224},{32,0},{64,32},{96,64},{128,96},{160,128},{192,160},{224,1... | collective-permute-start | bytes 491528 | tf_op jit(solution)/shard_map/ppermute | solution.py:226
  18.2 14.2 %collective-permute-start.5 = (f32[320,128]{1,0:T(8,128)S(1)}, f32[320,128]{1,0:T(8,128)S(1)}, u32[]{:S(2)}, u32[]{:S(2)}) collective-permute-start(f32[320,128]{1,0:T(8,128)S(1)} %get-tuple-element.29), channel_id=1, source_target_pairs={{0,192},{32,224},{64,0},{96,32},{128,64},{160,96},{192,128},{224,1... | collective-permute-start | bytes 491528 | tf_op jit(solution)/shard_map/ppermute | solution.py:226
  19.7 26.9 %collective-permute-start.4 = (f32[320,128]{1,0:T(8,128)S(1)}, f32[320,128]{1,0:T(8,128)S(1)}, u32[]{:S(2)}, u32[]{:S(2)}) collective-permute-start(f32[320,128]{1,0:T(8,128)S(1)} %get-tuple-element.30), channel_id=1, source_target_pairs={{0,160},{32,192},{64,224},{96,0},{128,32},{160,64},{192,96},{224,1... | collective-permute-start | bytes 491528 | tf_op jit(solution)/shard_map/ppermute | solution.py:226
  20.1 26.4 %collective-permute-start.3 = (f32[320,128]{1,0:T(8,128)S(1)}, f32[320,128]{1,0:T(8,128)S(1)}, u32[]{:S(2)}, u32[]{:S(2)}) collective-permute-start(f32[320,128]{1,0:T(8,128)S(1)} %get-tuple-element.31), channel_id=1, source_target_pairs={{0,128},{32,160},{64,192},{96,224},{128,0},{160,32},{192,64},{224,... | collective-permute-start | bytes 491528 | tf_op jit(solution)/shard_map/ppermute | solution.py:226
  25.1 22.6 %collective-permute-start.2 = (f32[320,128]{1,0:T(8,128)S(1)}, f32[320,128]{1,0:T(8,128)S(1)}, u32[]{:S(2)}, u32[]{:S(2)}) collective-permute-start(f32[320,128]{1,0:T(8,128)S(1)} %get-tuple-element.32), channel_id=1, source_target_pairs={{0,96},{32,128},{64,160},{96,192},{128,224},{160,0},{192,32},{224,... | collective-permute-start | bytes 491528 | tf_op jit(solution)/shard_map/ppermute | solution.py:226
  25.8 26.0 %collective-permute-start.1 = (f32[320,128]{1,0:T(8,128)S(1)}, f32[320,128]{1,0:T(8,128)S(1)}, u32[]{:S(2)}, u32[]{:S(2)}) collective-permute-start(f32[320,128]{1,0:T(8,128)S(1)} %get-tuple-element.33), channel_id=1, source_target_pairs={{0,64},{32,96},{64,128},{96,160},{128,192},{160,224},{192,0},{224,... | collective-permute-start | bytes 491528 | tf_op jit(solution)/shard_map/ppermute | solution.py:226
  32.4 21.8 %collective-permute-start = (f32[320,128]{1,0:T(8,128)S(1)}, f32[320,128]{1,0:T(8,128)S(1)}, u32[]{:S(2)}, u32[]{:S(2)}) collective-permute-start(f32[320,128]{1,0:T(8,128)S(1)} %get-tuple-element.34), channel_id=1, source_target_pairs={{0,32},{32,64},{64,96},{96,128},{128,160},{160,192},{192,224},{224... | collective-permute-start | bytes 491528 | tf_op jit(solution)/shard_map/ppermute | solution.py:226
  54.3 1.1 %copy-start = (f32[2560,128]{1,0:T(8,128)}, f32[2560,128]{1,0:T(8,128)S(1)}, u32[]{:S(2)}) copy-start(f32[2560,128]{1,0:T(8,128)S(1)} %join.1) | copy-start | bytes 3932164
  55.4 44.4 %all-to-all-start = ((f32[32,80,128]{2,1,0:T(8,128)}), f32[32,80,128]{2,1,0:T(8,128)S(1)}, u32[]{:S(2)}, u32[]{:S(2)}) async-start(f32[32,80,128]{2,1,0:T(8,128)} %bitcast.10), calls=%async_computation | async-start | bytes 2621440 | tf_op jit(solution)/shard_map/all_to_all | solution.py:283
  63.0 10.9 %collective-permute-start.7 = (f32[320,128]{1,0:T(8,128)S(1)}, f32[320,128]{1,0:T(8,128)S(1)}, u32[]{:S(2)}, u32[]{:S(2)}) collective-permute-start(f32[320,128]{1,0:T(8,128)S(1)} %get-tuple-element.17), channel_id=1, source_target_pairs={{0,32},{32,64},{64,96},{96,128},{128,160},{160,192},{192,224},{224... | collective-permute-start | bytes 491528 | tf_op jit(solution)/shard_map/ppermute | solution.py:226
  64.1 16.7 %collective-permute-start.8 = (f32[320,128]{1,0:T(8,128)S(1)}, f32[320,128]{1,0:T(8,128)S(1)}, u32[]{:S(2)}, u32[]{:S(2)}) collective-permute-start(f32[320,128]{1,0:T(8,128)S(1)} %get-tuple-element.18), channel_id=1, source_target_pairs={{0,64},{32,96},{64,128},{96,160},{128,192},{160,224},{192,0},{224,... | collective-permute-start | bytes 491528 | tf_op jit(solution)/shard_map/ppermute | solution.py:226
  65.1 25.9 %collective-permute-start.9 = (f32[320,128]{1,0:T(8,128)S(1)}, f32[320,128]{1,0:T(8,128)S(1)}, u32[]{:S(2)}, u32[]{:S(2)}) collective-permute-start(f32[320,128]{1,0:T(8,128)S(1)} %get-tuple-element.19), channel_id=1, source_target_pairs={{0,96},{32,128},{64,160},{96,192},{128,224},{160,0},{192,32},{224,... | collective-permute-start | bytes 491528 | tf_op jit(solution)/shard_map/ppermute | solution.py:226
  66.7 24.3 %collective-permute-start.10 = (f32[320,128]{1,0:T(8,128)S(1)}, f32[320,128]{1,0:T(8,128)S(1)}, u32[]{:S(2)}, u32[]{:S(2)}) collective-permute-start(f32[320,128]{1,0:T(8,128)S(1)} %get-tuple-element.20), channel_id=1, source_target_pairs={{0,128},{32,160},{64,192},{96,224},{128,0},{160,32},{192,64},{224,... | collective-permute-start | bytes 491528 | tf_op jit(solution)/shard_map/ppermute | solution.py:226
  71.5 19.5 %collective-permute-start.11 = (f32[320,128]{1,0:T(8,128)S(1)}, f32[320,128]{1,0:T(8,128)S(1)}, u32[]{:S(2)}, u32[]{:S(2)}) collective-permute-start(f32[320,128]{1,0:T(8,128)S(1)} %get-tuple-element.21), channel_id=1, source_target_pairs={{0,160},{32,192},{64,224},{96,0},{128,32},{160,64},{192,96},{224,1... | collective-permute-start | bytes 491528 | tf_op jit(solution)/shard_map/ppermute | solution.py:226
  73.9 22.5 %collective-permute-start.12 = (f32[320,128]{1,0:T(8,128)S(1)}, f32[320,128]{1,0:T(8,128)S(1)}, u32[]{:S(2)}, u32[]{:S(2)}) collective-permute-start(f32[320,128]{1,0:T(8,128)S(1)} %get-tuple-element.22), channel_id=1, source_target_pairs={{0,192},{32,224},{64,0},{96,32},{128,64},{160,96},{192,128},{224,1... | collective-permute-start | bytes 491528 | tf_op jit(solution)/shard_map/ppermute | solution.py:226
  80.8 19.0 %collective-permute-start.13 = (f32[320,128]{1,0:T(8,128)S(1)}, f32[320,128]{1,0:T(8,128)S(1)}, u32[]{:S(2)}, u32[]{:S(2)}) collective-permute-start(f32[320,128]{1,0:T(8,128)S(1)} %get-tuple-element.23), channel_id=1, source_target_pairs={{0,224},{32,0},{64,32},{96,64},{128,96},{160,128},{192,160},{224,1... | collective-permute-start | bytes 491528 | tf_op jit(solution)/shard_map/ppermute | solution.py:226

commit v4 on v3

--- a/solution.py
+++ b/solution.py
@@ -62,7 +62,8 @@
     return out
 
 
-def pack(coef_ref, bands_ref, wh_hbm, wl_hbm, one_ref, two_ref, cbuf, buf, wh_ref, wl_ref, spec, sems):
+def pack(coef_ref, bands_ref, wh_hbm, wl_hbm, *refs):
+    out_one, out_two, (one_ref, two_ref, cbuf, buf, wh_ref, wl_ref, spec, sems) = refs[:ZD], refs[ZD], refs[ZD + 1 :]
     halves = [pl.ds(h * LANES, LANES) for h in range(2)]
     mine = lax.axis_index("y")
     turn_by = [lax.rem(k + 4 - mine, 4) for k in range(4)]
@@ -79,20 +80,17 @@
     for copy in starts + sum(copies, []):
         copy.start()
 
-    def turn(b):
+    def turn(b, yh):
         for xh in range(2):
-            for yh in range(2):
-                block = jnp.concatenate(
-                    [buf[b, xh, pl.ds(yh * 4 + turn_by[k], ZL, stride=YL), :] for k in range(4)]
-                )
-                turned = block.T
-                for r in range(16):
-                    hop, place = hops[xh * 4 + r // 4], r % 4 * COLS + b
-                    value = turned[r * 8 : r * 8 + 8]
-                    if yh == 0:
-                        one_ref[pl.ds(pl.multiple_of(hop * PIECE + place * 8, 8), 8), :] = value
-                    else:
-                        two_ref[pl.ds(pl.multiple_of(place * SLOT + hop * 8, 8), 8), :] = value
+            block = jnp.concatenate([buf[b, xh, pl.ds(yh * 4 + turn_by[k], ZL, stride=YL), :] for k in range(4)])
+            turned = block.T
+            for r in range(16):
+                hop, place = hops[xh * 4 + r // 4], r % 4 * COLS + b
+                value = turned[r * 8 : r * 8 + 8]
+                if yh == 0:
+                    one_ref[pl.ds(pl.multiple_of(hop * PIECE + place * 8, 8), 8), :] = value
+                else:
+                    two_ref[pl.ds(pl.multiple_of(place * SLOT + hop * 8, 8), 8), :] = value
 
     for step, bands in enumerate(STEPS):
         for b in bands:
@@ -115,24 +113,42 @@
                 spec[h, pl.ds(0, N), :] = q[:N, one] - q[N:, two]
                 spec[h, pl.ds(N, N), :] = q[N:, one] + q[:N, two]
         for b in bands:
-            turn(b)
+            turn(b, 0)
     for b in range(BANDS):
         for yh in range(2):
             for z in range(ZD):
-                for part in range(2):
-                    value = spec[yh, pl.ds(part * N + z * 32 + b, 4, stride=8), :]
-                    if part == 0:
-                        one_ref[pl.ds(hops[z] * PIECE + 8 * PLANE + yh * PLANE + b, 4, stride=COLS), :] = value
-                    else:
-                        two_ref[pl.ds(b * SLOT + 8 * ZD + hops[z] * 2 + yh, 4, stride=COLS * SLOT), :] = value
+                one_ref[pl.ds(hops[z] * PIECE + 8 * PLANE + yh * PLANE + b, 4, stride=COLS), :] = spec[
+                    yh, pl.ds(z * 32 + b, 4, stride=8), :
+                ]
+    out = [
+        pltpu.make_async_copy(one_ref.at[pl.ds(k * PIECE, PIECE)], out_one[k], sems.at[4 + 2 * BANDS + k])
+        for k in range(ZD)
+    ]
+    for copy in out:
+        copy.start()
+    for b in range(BANDS):
+        turn(b, 1)
+        for yh in range(2):
+            for z in range(ZD):
+                two_ref[pl.ds(b * SLOT + 8 * ZD + hops[z] * 2 + yh, 4, stride=COLS * SLOT), :] = spec[
+                    yh, pl.ds(N + z * 32 + b, 4, stride=8), :
+                ]
+    out.append(pltpu.make_async_copy(two_ref, out_two, sems.at[4 + 2 * BANDS + ZD]))
+    out[-1].start()
+    for copy in out:
+        copy.wait()
 
 
 STEPS = ((0, 1, 2, 3), (4, 5, 6, 7))
 DFT_AT = 0
 
 
-def regroup(in_ref, *out_refs):
-    for k, out_ref in enumerate(out_refs):
+def regroup(in_ref, *refs):
+    out_refs, held, sems = refs[:ZD], refs[ZD], refs[ZD + 1]
+    late = HOPS[AHEAD:]
+    copies = []
+    for k in late + tuple(k for k in range(ZD) if k not in late):
+        out_ref = held.at[late.index(k)] if k in late else out_refs[k]
         for p in range(PLANE):
             out_ref[pl.ds(p * 8, 8), :] = in_ref[pl.ds(p * SLOT + k * 8, 8), :]
         for j in range(2):
@@ -140,6 +156,11 @@
                 out_ref[pl.ds(PLANE * 8 + j * PLANE + g * 8, 8), :] = in_ref[
                     pl.ds(g * 8 * SLOT + 8 * ZD + k * 2 + j, 8, stride=SLOT), :
                 ]
+        if k in late:
+            copies.append(pltpu.make_async_copy(out_ref, out_refs[k], sems.at[late.index(k)]))
+            copies[-1].start()
+    for copy in copies:
+        copy.wait()
 
 
 def join(*refs):
@@ -152,6 +173,9 @@
                 out_ref[pl.ds(g * 8 * SLOT + 8 * ZD + k * 2 + j, 8, stride=SLOT), :] = in_ref[
                     pl.ds(PLANE * 8 + j * PLANE + g * 8, 8), :
                 ]
+
+
+BEFORE = 6
 
 
 def unpack(*refs):
@@ -169,30 +193,15 @@
     for k in range(ZD):
         for part in range(2):
             for yh in range(2):
-                for h in range(2):
-                    if part == 0:
-                        first = h * 4 * SLOT + 8 * ZD + k * 2 + yh
-                        vs = [one_ref[pl.ds(first + c * SLOT, 4, stride=COLS * SLOT), :] for c in range(4)]
-                    else:
-                        first = PLANE * 8 + yh * PLANE + h * 4
-                        vs = [two_refs[k][pl.ds(first + c, 4, stride=COLS), :] for c in range(4)]
-                    for y, v in enumerate(exchange_blocks(vs)):
-                        field[h, pl.ds(part * N + source[k] * 8 + yh * 4 + y, 4, stride=64), :] = v
-    for fetch in fetches:
-        fetch.wait()
-    values = jnp.concatenate([field[0], field[1]], axis=1)
-    q = product(yh_ref[...], yl_ref[...], jnp.concatenate([values[:N], values[N:]], axis=1), ((1,), (0,)))
-    along = jnp.concatenate([q[:N, :N] - q[N:, N:], q[N:, :N] + q[:N, N:]])
-    q = product(wh_ref[...], wl_ref[...], along, ((1,), (1,)))
-    real = q[:N, :N] - q[N:, N:]
-    imag = q[N:, :N] + q[:N, N:]
-    for h in range(2):
-        lanes = slice(h * LANES, (h + 1) * LANES)
-        cout[pl.ds(h, N, stride=2), :] = real[:, lanes]
-        cout[pl.ds(2 * N + h, N, stride=2), :] = imag[:, lanes]
-    copies = [pltpu.make_async_copy(cout, coefs_ref, sems.at[2 * ZD])]
-    copies[0].start()
-    for k in range(ZD):
+                if part == 0:
+                    vs = [one_ref[pl.ds(c * SLOT + 8 * ZD + k * 2 + yh, 8, stride=4 * SLOT), :] for c in range(4)]
+                else:
+                    vs = [two_refs[k][pl.ds(PLANE * 8 + yh * PLANE + c, 8, stride=4), :] for c in range(4)]
+                for y, v in enumerate(exchange_blocks(vs)):
+                    field[pl.ds(part * 2 * N + source[k] * 8 + yh * 4 + y, 8, stride=64), :] = v
+    copies = []
+
+    def place(k):
         for h in range(2):
             for r in range(4):
                 for yh in range(2):
@@ -210,6 +219,32 @@
                 )
             )
             copies[-1].start()
+
+    for k in range(BEFORE):
+        place(k)
+    for fetch in fetches:
+        fetch.wait()
+    values = jnp.concatenate(
+        [
+            jnp.concatenate([field[pl.ds(part * 2 * N + r * 128 + h * 64, 64), :] for r in range(4)])
+            for part in range(2)
+            for h in range(2)
+        ],
+        axis=1,
+    )
+    q = product(yh_ref[...], yl_ref[...], values, ((1,), (0,)))
+    along = jnp.concatenate([q[:N, :N] - q[N:, N:], q[N:, :N] + q[:N, N:]])
+    q = product(wh_ref[...], wl_ref[...], along, ((1,), (1,)))
+    real = q[:N, :N] - q[N:, N:]
+    imag = q[N:, :N] + q[:N, N:]
+    for h in range(2):
+        lanes = slice(h * LANES, (h + 1) * LANES)
+        cout[pl.ds(h, N, stride=2), :] = real[:, lanes]
+        cout[pl.ds(2 * N + h, N, stride=2), :] = imag[:, lanes]
+    copies.append(pltpu.make_async_copy(cout, coefs_ref, sems.at[2 * ZD]))
+    copies[-1].start()
+    for k in range(BEFORE, ZD):
+        place(k)
     for copy in copies:
         copy.wait()
 
@@ -228,6 +263,7 @@
 
 
 HOPS = (3, 5, 4, 2, 6, 1, 7)
+AHEAD = 3
 
 
 def local(coefficients, real_bands):
@@ -235,22 +271,21 @@
     assert real_bands.shape == (BANDS, ZL, YL, N)
     wh, wl, yh, yl = (jnp.asarray(t) for t in tables())
     params = pltpu.CompilerParams(vmem_limit_bytes=16 << 20)
-    one, two = pl.pallas_call(
+    *one, two = pl.pallas_call(
         pack,
         name="pack",
-        out_shape=[
-            jax.ShapeDtypeStruct((ZD * PIECE, LANES), f32),
-            jax.ShapeDtypeStruct((PLANE * SLOT, LANES), f32),
-        ],
+        out_shape=[jax.ShapeDtypeStruct((PIECE, LANES), f32)] * ZD + [jax.ShapeDtypeStruct((PLANE * SLOT, LANES), f32)],
         in_specs=[anywhere] * 4,
-        out_specs=[vmem, vmem],
+        out_specs=[anywhere] * (ZD + 1),
         scratch_shapes=[
+            pltpu.VMEM((ZD * PIECE, LANES), f32),
+            pltpu.VMEM((PLANE * SLOT, LANES), f32),
             pltpu.VMEM((2, 2 * ZL * YL, LANES), f32),
             pltpu.VMEM((BANDS, 2, ZL * YL, LANES), f32),
             pltpu.VMEM((2 * N, N), bf16),
             pltpu.VMEM((2 * N, N), bf16),
             pltpu.VMEM((2, 2 * N, LANES), f32),
-            pltpu.SemaphoreType.DMA((4 + 2 * BANDS,)),
+            pltpu.SemaphoreType.DMA((5 + 2 * BANDS + ZD,)),
         ],
         compiler_params=params,
     )(
@@ -260,14 +295,17 @@
         pltpu.with_memory_space_constraint(wl, pltpu.HBM),
     )
     two = lax.all_to_all(two.reshape(PLANE, SLOT, LANES), plane, split_axis=0, concat_axis=0, tiled=True)
-    one = one.reshape(ZD, PIECE, LANES)
-    one = by_hop([one[k] for k in range(ZD)])
+    one = by_hop(one)
     parts = pl.pallas_call(
         regroup,
         name="regroup",
-        out_shape=[jax.ShapeDtypeStruct((PIECE, LANES), f32)] * ZD,
+        out_shape=[(pltpu.HBM if k in HOPS[AHEAD:] else pltpu.VMEM)((PIECE, LANES), f32) for k in range(ZD)],
         in_specs=[vmem],
-        out_specs=[vmem] * ZD,
+        out_specs=[anywhere if k in HOPS[AHEAD:] else vmem for k in range(ZD)],
+        scratch_shapes=[
+            pltpu.VMEM((len(HOPS) - AHEAD, PIECE, LANES), f32),
+            pltpu.SemaphoreType.DMA((len(HOPS) - AHEAD,)),
+        ],
         compiler_params=params,
     )(two.reshape(PLANE * SLOT, LANES))
     parts = by_hop(parts)
@@ -294,7 +332,7 @@
             *[pltpu.VMEM((2 * N, N), bf16)] * 4,
             pltpu.VMEM((4 * N, LANES), f32),
             pltpu.VMEM((2, XL, N + 8, LANES), f32),
-            pltpu.VMEM((2, 2 * N, LANES), f32),
+            pltpu.VMEM((4 * N, LANES), f32),
             pltpu.SemaphoreType.DMA((2 * ZD + 5,)),
         ],
         compiler_params=params,

time: 107 us -> 109 us (1.019)
  starting transfers between devices: 40 us -> 49 us
  waiting for transfers between devices: 53.6 us -> 45 us
  Pallas kernels: 10 us -> 12.1 us
    ppermute x14, starting transfers between devices: 25.1 us -> 34 us  [by_hop(): out[k] = lax.ppermute(values[k], 'z', shift[k])]
    ppermute x14, waiting for transfers between devices: 53.6 us -> 45 us  [by_hop(): out[k] = lax.ppermute(values[k], 'z', shift[k])]
    pallas_call x2, Pallas kernels: 4.13 us -> 7.15 us  [the longest x1 6.28 us: local(): pl.pallas_call(pack, name='pack', out_shape=[jax.ShapeDtypeStruct((PIECE,...]
  transfers between devices with their start and end apart: 16 -> 16, of which waited for: 11 -> 10; matrix products, arithmetic and copies ran while one was open for 0% -> 0% of each run, Pallas kernels for 0% -> 1%
where the time goes in v4:
time: 109 us; the launch traced here: 108 us
  starting transfers between devices  49 us (45%)
  waiting for transfers between devices  45 us (41%)
  Pallas kernels  12.1 us (11%)
    ppermute x14, waiting for transfers between devices, by_hop(): out[k] = lax.ppermute(values[k], 'z', shift[k])  45 us
    ppermute x14, starting transfers between devices, by_hop(): out[k] = lax.ppermute(values[k], 'z', shift[k])  34 us
    all_to_all x1, starting transfers between devices, local(): lax.all_to_all(two.reshape(PLANE, SLOT, LANES), plane, split_axis=0, conc...  7.55 us
    all_to_all x1, starting transfers between devices, local(): one = lax.all_to_all(one, plane, split_axis=0, concat_axis=0, tiled=True)  7.42 us
    pallas_call x1, Pallas kernels, local(): pl.pallas_call(pack, name='pack', out_shape=[jax.ShapeDtypeStruct((PIECE,...  6.28 us
    pallas_call x1, Pallas kernels, local(): pl.pallas_call(unpack, name='unpack', out_shape=[jax.ShapeDtypeStruct((4...  4.77 us
  transfers between devices with their start and end apart: 16, of which 10 were waited for; matrix products, arithmetic and copies ran while one was open for 0% of the time, Pallas kernels for 1%

profile of v4, /device:TPU:8, one launch (start us, length us, event | category | flops | bytes accessed | tf_op | source)
XLA Modules:
  0.0 108.0 jit_solution(4701337181995772330)
XLA Ops:
  0.6 6.3 %pack.1 = (f32[320,128]{1,0:T(8,128)S(1)}, f32[320,128]{1,0:T(8,128)S(1)}, f32[320,128]{1,0:T(8,128)S(1)}, f32[320,128]{1,0:T(8,128)S(1)}, f32[320,128]{1,0:T(8,...) custom-call(f32[512,256]{1,0:T(8,128)} %bitcast.12, ...), custom_call_target="tpu_custom_call" | custom-call | tf_op jit(solution)/shard_map/pack/pallas_call | solution.py:274
  6.9 7.5 %all-to-all-start.1 = ((f32[32,80,128]{2,1,0:T(8,128)}), f32[32,80,128]{2,1,0:T(8,128)S(1)}, u32[]{:S(2)}, u32[]{:S(2)}) async-start(f32[32,80,128]{2,1,0:T(8,128)} %bitcast.4), calls=%async_computation.1 | async-start | bytes 2621440 | tf_op jit(solution)/shard_map/all_to_all | solution.py:297
  14.5 2.0 %collective-permute-start = (f32[320,128]{1,0:T(8,128)S(1)}, f32[320,128]{1,0:T(8,128)S(1)}, u32[]{:S(2)}, u32[]{:S(2)}) collective-permute-start(f32[320,128]{1,0:T(8,128)S(1)} %get-tuple-element.22), channel_id=1, source_target_pairs={{0,32},{32,64},{64,96},{96,128},{128,160},{160,192},{192,224},{224... | collective-permute-start | bytes 491528 | tf_op jit(solution)/shard_map/ppermute | solution.py:261
  16.5 3.3 %collective-permute-start.1 = (f32[320,128]{1,0:T(8,128)S(1)}, f32[320,128]{1,0:T(8,128)S(1)}, u32[]{:S(2)}, u32[]{:S(2)}) collective-permute-start(f32[320,128]{1,0:T(8,128)S(1)} %get-tuple-element.23), channel_id=1, source_target_pairs={{0,64},{32,96},{64,128},{96,160},{128,192},{160,224},{192,0},{224,... | collective-permute-start | bytes 491528 | tf_op jit(solution)/shard_map/ppermute | solution.py:261
  19.7 4.0 %collective-permute-start.2 = (f32[320,128]{1,0:T(8,128)S(1)}, f32[320,128]{1,0:T(8,128)S(1)}, u32[]{:S(2)}, u32[]{:S(2)}) collective-permute-start(f32[320,128]{1,0:T(8,128)S(1)} %get-tuple-element.24), channel_id=1, source_target_pairs={{0,96},{32,128},{64,160},{96,192},{128,224},{160,0},{192,32},{224,... | collective-permute-start | bytes 491528 | tf_op jit(solution)/shard_map/ppermute | solution.py:261
  23.8 0.5 collective-permute-start.3
  24.3 4.9 %collective-permute-start.4 = (f32[320,128]{1,0:T(8,128)S(1)}, f32[320,128]{1,0:T(8,128)S(1)}, u32[]{:S(2)}, u32[]{:S(2)}) collective-permute-start(f32[320,128]{1,0:T(8,128)S(1)} %get-tuple-element.26), channel_id=1, source_target_pairs={{0,160},{32,192},{64,224},{96,0},{128,32},{160,64},{192,96},{224,1... | collective-permute-start | bytes 491528 | tf_op jit(solution)/shard_map/ppermute | solution.py:261
  29.3 0.0 collective-permute-done.refs_1_
  29.3 2.7 %collective-permute-start.5 = (f32[320,128]{1,0:T(8,128)S(1)}, f32[320,128]{1,0:T(8,128)S(1)}, u32[]{:S(2)}, u32[]{:S(2)}) collective-permute-start(f32[320,128]{1,0:T(8,128)S(1)} %get-tuple-element.27), channel_id=1, source_target_pairs={{0,192},{32,224},{64,0},{96,32},{128,64},{160,96},{192,128},{224,1... | collective-permute-start | bytes 491528 | tf_op jit(solution)/shard_map/ppermute | solution.py:261
  31.9 3.2 %collective-permute-done.1.refs_2_ = f32[320,128]{1,0:T(8,128)S(1)} collective-permute-done((f32[320,128]{1,0:T(8,128)S(1)}, f32[320,128]{1,0:T(8,128)S(1)}, u32[]{:S(2)}, u32[]{:S(2)}) %collective-permute-start.1) | collective-permute-done | bytes 163872 | tf_op jit(solution)/shard_map/ppermute | solution.py:261
  35.1 2.6 %collective-permute-start.6 = (f32[320,128]{1,0:T(8,128)S(1)}, f32[320,128]{1,0:T(8,128)S(1)}, u32[]{:S(2)}, u32[]{:S(2)}) collective-permute-start(f32[320,128]{1,0:T(8,128)S(1)} %get-tuple-element.28), channel_id=1, source_target_pairs={{0,224},{32,0},{64,32},{96,64},{128,96},{160,128},{192,160},{224,1... | collective-permute-start | bytes 491528 | tf_op jit(solution)/shard_map/ppermute | solution.py:261
  37.7 8.5 %collective-permute-done.2.refs_3_ = f32[320,128]{1,0:T(8,128)S(1)} collective-permute-done((f32[320,128]{1,0:T(8,128)S(1)}, f32[320,128]{1,0:T(8,128)S(1)}, u32[]{:S(2)}, u32[]{:S(2)}) %collective-permute-start.2) | collective-permute-done | bytes 163872 | tf_op jit(solution)/shard_map/ppermute | solution.py:261
  46.2 0.0 collective-permute-done.3.refs_4_
  46.2 2.2 %collective-permute-done.4.refs_5_ = f32[320,128]{1,0:T(8,128)S(1)} collective-permute-done((f32[320,128]{1,0:T(8,128)S(1)}, f32[320,128]{1,0:T(8,128)S(1)}, u32[]{:S(2)}, u32[]{:S(2)}) %collective-permute-start.4) | collective-permute-done | bytes 163872 | tf_op jit(solution)/shard_map/ppermute | solution.py:261
  48.3 4.8 %collective-permute-done.5.refs_6_ = f32[320,128]{1,0:T(8,128)S(1)} collective-permute-done((f32[320,128]{1,0:T(8,128)S(1)}, f32[320,128]{1,0:T(8,128)S(1)}, u32[]{:S(2)}, u32[]{:S(2)}) %collective-permute-start.5) | collective-permute-done | bytes 163872 | tf_op jit(solution)/shard_map/ppermute | solution.py:261
  53.2 1.1 %collective-permute-done.6.refs_7_ = f32[320,128]{1,0:T(8,128)S(1)} collective-permute-done((f32[320,128]{1,0:T(8,128)S(1)}, f32[320,128]{1,0:T(8,128)S(1)}, u32[]{:S(2)}, u32[]{:S(2)}) %collective-permute-start.6) | collective-permute-done | bytes 163872 | tf_op jit(solution)/shard_map/ppermute | solution.py:261
  54.3 0.2 join.1
  54.4 0.0 copy-start
  54.5 1.1 copy-done
  55.5 0.0 all-to-all-done.1
  55.5 7.4 %all-to-all-start = ((f32[32,80,128]{2,1,0:T(8,128)}), f32[32,80,128]{2,1,0:T(8,128)S(1)}, u32[]{:S(2)}, u32[]{:S(2)}) async-start(f32[32,80,128]{2,1,0:T(8,128)} %bitcast.10), calls=%async_computation | async-start | bytes 2621440 | tf_op jit(solution)/shard_map/all_to_all | solution.py:321
  63.0 0.9 regroup.1
  63.8 3.6 %collective-permute-start.7 = (f32[320,128]{1,0:T(8,128)}, f32[320,128]{1,0:T(8,128)S(1)}, u32[]{:S(2)}, u32[]{:S(2)}) collective-permute-start(f32[320,128]{1,0:T(8,128)} %get-tuple-element.31), channel_id=1, source_target_pairs={{0,32},{32,64},{64,96},{96,128},{128,160},{160,192},{192,224},{224... | collective-permute-start | bytes 491528 | tf_op jit(solution)/shard_map/ppermute | solution.py:261
  67.5 1.1 %collective-permute-start.8 = (f32[320,128]{1,0:T(8,128)}, f32[320,128]{1,0:T(8,128)S(1)}, u32[]{:S(2)}, u32[]{:S(2)}) collective-permute-start(f32[320,128]{1,0:T(8,128)} %get-tuple-element.32), channel_id=1, source_target_pairs={{0,64},{32,96},{64,128},{96,160},{128,192},{160,224},{192,0},{224,... | collective-permute-start | bytes 491528 | tf_op jit(solution)/shard_map/ppermute | solution.py:261
  68.6 0.6 collective-permute-start.9
  69.2 4.7 %collective-permute-start.10 = (f32[320,128]{1,0:T(8,128)S(1)}, f32[320,128]{1,0:T(8,128)S(1)}, u32[]{:S(2)}, u32[]{:S(2)}) collective-permute-start(f32[320,128]{1,0:T(8,128)S(1)} %get-tuple-element.34), channel_id=1, source_target_pairs={{0,128},{32,160},{64,192},{96,224},{128,0},{160,32},{192,64},{224,... | collective-permute-start | bytes 491528 | tf_op jit(solution)/shard_map/ppermute | solution.py:261
  73.9 1.5 %collective-permute-start.11 = (f32[320,128]{1,0:T(8,128)S(1)}, f32[320,128]{1,0:T(8,128)S(1)}, u32[]{:S(2)}, u32[]{:S(2)}) collective-permute-start(f32[320,128]{1,0:T(8,128)S(1)} %get-tuple-element.35), channel_id=1, source_target_pairs={{0,160},{32,192},{64,224},{96,0},{128,32},{160,64},{192,96},{224,1... | collective-permute-start | bytes 491528 | tf_op jit(solution)/shard_map/ppermute | solution.py:261
  75.4 0.0 collective-permute-done.7.refs_2_
  75.4 2.4 %collective-permute-start.12 = (f32[320,128]{1,0:T(8,128)}, f32[320,128]{1,0:T(8,128)S(1)}, u32[]{:S(2)}, u32[]{:S(2)}) collective-permute-start(f32[320,128]{1,0:T(8,128)} %get-tuple-element.36), channel_id=1, source_target_pairs={{0,192},{32,224},{64,0},{96,32},{128,64},{160,96},{192,128},{224,1... | collective-permute-start | bytes 491528 | tf_op jit(solution)/shard_map/ppermute | solution.py:261
  77.8 6.7 %collective-permute-done.8.refs_3_ = f32[320,128]{1,0:T(8,128)S(1)} collective-permute-done((f32[320,128]{1,0:T(8,128)}, f32[320,128]{1,0:T(8,128)S(1)}, u32[]{:S(2)}, u32[]{:S(2)}) %collective-permute-start.8) | collective-permute-done | bytes 163872 | tf_op jit(solution)/shard_map/ppermute | solution.py:261
  84.5 0.0 collective-permute-start.13
  84.5 6.0 %collective-permute-done.9.refs_4_ = f32[320,128]{1,0:T(8,128)S(1)} collective-permute-done((f32[320,128]{1,0:T(8,128)S(1)}, f32[320,128]{1,0:T(8,128)S(1)}, u32[]{:S(2)}, u32[]{:S(2)}) %collective-permute-start.9) | collective-permute-done | bytes 163872 | tf_op jit(solution)/shard_map/ppermute | solution.py:261
  90.5 5.6 %collective-permute-done.10.refs_5_ = f32[320,128]{1,0:T(8,128)S(1)} collective-permute-done((f32[320,128]{1,0:T(8,128)S(1)}, f32[320,128]{1,0:T(8,128)S(1)}, u32[]{:S(2)}, u32[]{:S(2)}) %collective-permute-start.10) | collective-permute-done | bytes 163872 | tf_op jit(solution)/shard_map/ppermute | solution.py:261
  96.1 0.0 collective-permute-done.11.refs_6_
  96.1 3.5 %collective-permute-done.12.refs_7_ = f32[320,128]{1,0:T(8,128)S(1)} collective-permute-done((f32[320,128]{1,0:T(8,128)}, f32[320,128]{1,0:T(8,128)S(1)}, u32[]{:S(2)}, u32[]{:S(2)}) %collective-permute-start.12) | collective-permute-done | bytes 163872 | tf_op jit(solution)/shard_map/ppermute | solution.py:261
  99.6 3.5 %collective-permute-done.13.refs_8_ = f32[320,128]{1,0:T(8,128)S(1)} collective-permute-done((f32[320,128]{1,0:T(8,128)}, f32[320,128]{1,0:T(8,128)S(1)}, u32[]{:S(2)}, u32[]{:S(2)}) %collective-permute-start.13) | collective-permute-done | bytes 163872 | tf_op jit(solution)/shard_map/ppermute | solution.py:261
  103.1 0.0 all-to-all-done
  103.1 4.8 %unpack.1 = (f32[1024,128]{1,0:T(8,128)}, f32[8,256,256]{2,1,0:T(8,128)}) custom-call(f32[2560,128]{1,0:T(8,128)S(1)} %bitcast.8, f32[320,128]{1,0:T(8,128)S(1)} %get-tuple-element.30.refs_1_, f32[320,128]{1,0:T(8,128)S(1)} %collective-permute-done.7.refs_2_, f32[320,128]{1,0:T(8,128)S(1)} %collective-permute-done.8.refs_3_, ...), custom_call_target="tpu_custom_call" | custom-call | tf_op jit(solution)/shard_map/unpack/pallas_call | solution.py:322
Async XLA Ops:
  6.9 48.6 %all-to-all-start.1 = ((f32[32,80,128]{2,1,0:T(8,128)}), f32[32,80,128]{2,1,0:T(8,128)S(1)}, u32[]{:S(2)}, u32[]{:S(2)}) async-start(f32[32,80,128]{2,1,0:T(8,128)} %bitcast.4), calls=%async_computation.1 | async-start | bytes 2621440 | tf_op jit(solution)/shard_map/all_to_all | solution.py:297
  14.5 14.8 %collective-permute-start = (f32[320,128]{1,0:T(8,128)S(1)}, f32[320,128]{1,0:T(8,128)S(1)}, u32[]{:S(2)}, u32[]{:S(2)}) collective-permute-start(f32[320,128]{1,0:T(8,128)S(1)} %get-tuple-element.22), channel_id=1, source_target_pairs={{0,32},{32,64},{64,96},{96,128},{128,160},{160,192},{192,224},{224... | collective-permute-start | bytes 491528 | tf_op jit(solution)/shard_map/ppermute | solution.py:261
  16.5 18.6 %collective-permute-start.1 = (f32[320,128]{1,0:T(8,128)S(1)}, f32[320,128]{1,0:T(8,128)S(1)}, u32[]{:S(2)}, u32[]{:S(2)}) collective-permute-start(f32[320,128]{1,0:T(8,128)S(1)} %get-tuple-element.23), channel_id=1, source_target_pairs={{0,64},{32,96},{64,128},{96,160},{128,192},{160,224},{192,0},{224,... | collective-permute-start | bytes 491528 | tf_op jit(solution)/shard_map/ppermute | solution.py:261
  19.7 26.4 %collective-permute-start.2 = (f32[320,128]{1,0:T(8,128)S(1)}, f32[320,128]{1,0:T(8,128)S(1)}, u32[]{:S(2)}, u32[]{:S(2)}) collective-permute-start(f32[320,128]{1,0:T(8,128)S(1)} %get-tuple-element.24), channel_id=1, source_target_pairs={{0,96},{32,128},{64,160},{96,192},{128,224},{160,0},{192,32},{224,... | collective-permute-start | bytes 491528 | tf_op jit(solution)/shard_map/ppermute | solution.py:261
  23.8 22.4 %collective-permute-start.3 = (f32[320,128]{1,0:T(8,128)S(1)}, f32[320,128]{1,0:T(8,128)S(1)}, u32[]{:S(2)}, u32[]{:S(2)}) collective-permute-start(f32[320,128]{1,0:T(8,128)S(1)} %get-tuple-element.25), channel_id=1, source_target_pairs={{0,128},{32,160},{64,192},{96,224},{128,0},{160,32},{192,64},{224,... | collective-permute-start | bytes 491528 | tf_op jit(solution)/shard_map/ppermute | solution.py:261
  24.3 24.0 %collective-permute-start.4 = (f32[320,128]{1,0:T(8,128)S(1)}, f32[320,128]{1,0:T(8,128)S(1)}, u32[]{:S(2)}, u32[]{:S(2)}) collective-permute-start(f32[320,128]{1,0:T(8,128)S(1)} %get-tuple-element.26), channel_id=1, source_target_pairs={{0,160},{32,192},{64,224},{96,0},{128,32},{160,64},{192,96},{224,1... | collective-permute-start | bytes 491528 | tf_op jit(solution)/shard_map/ppermute | solution.py:261
  29.3 23.9 %collective-permute-start.5 = (f32[320,128]{1,0:T(8,128)S(1)}, f32[320,128]{1,0:T(8,128)S(1)}, u32[]{:S(2)}, u32[]{:S(2)}) collective-permute-start(f32[320,128]{1,0:T(8,128)S(1)} %get-tuple-element.27), channel_id=1, source_target_pairs={{0,192},{32,224},{64,0},{96,32},{128,64},{160,96},{192,128},{224,1... | collective-permute-start | bytes 491528 | tf_op jit(solution)/shard_map/ppermute | solution.py:261
  35.1 19.2 %collective-permute-start.6 = (f32[320,128]{1,0:T(8,128)S(1)}, f32[320,128]{1,0:T(8,128)S(1)}, u32[]{:S(2)}, u32[]{:S(2)}) collective-permute-start(f32[320,128]{1,0:T(8,128)S(1)} %get-tuple-element.28), channel_id=1, source_target_pairs={{0,224},{32,0},{64,32},{96,64},{128,96},{160,128},{192,160},{224,1... | collective-permute-start | bytes 491528 | tf_op jit(solution)/shard_map/ppermute | solution.py:261
  54.4 1.1 copy-start
  55.5 47.6 %all-to-all-start = ((f32[32,80,128]{2,1,0:T(8,128)}), f32[32,80,128]{2,1,0:T(8,128)S(1)}, u32[]{:S(2)}, u32[]{:S(2)}) async-start(f32[32,80,128]{2,1,0:T(8,128)} %bitcast.10), calls=%async_computation | async-start | bytes 2621440 | tf_op jit(solution)/shard_map/all_to_all | solution.py:321
  63.8 11.6 %collective-permute-start.7 = (f32[320,128]{1,0:T(8,128)}, f32[320,128]{1,0:T(8,128)S(1)}, u32[]{:S(2)}, u32[]{:S(2)}) collective-permute-start(f32[320,128]{1,0:T(8,128)} %get-tuple-element.31), channel_id=1, source_target_pairs={{0,32},{32,64},{64,96},{96,128},{128,160},{160,192},{192,224},{224... | collective-permute-start | bytes 491528 | tf_op jit(solution)/shard_map/ppermute | solution.py:261
  67.5 17.0 %collective-permute-start.8 = (f32[320,128]{1,0:T(8,128)}, f32[320,128]{1,0:T(8,128)S(1)}, u32[]{:S(2)}, u32[]{:S(2)}) collective-permute-start(f32[320,128]{1,0:T(8,128)} %get-tuple-element.32), channel_id=1, source_target_pairs={{0,64},{32,96},{64,128},{96,160},{128,192},{160,224},{192,0},{224,... | collective-permute-start | bytes 491528 | tf_op jit(solution)/shard_map/ppermute | solution.py:261
  68.6 21.9 %collective-permute-start.9 = (f32[320,128]{1,0:T(8,128)S(1)}, f32[320,128]{1,0:T(8,128)S(1)}, u32[]{:S(2)}, u32[]{:S(2)}) collective-permute-start(f32[320,128]{1,0:T(8,128)S(1)} %get-tuple-element.33), channel_id=1, source_target_pairs={{0,96},{32,128},{64,160},{96,192},{128,224},{160,0},{192,32},{224,... | collective-permute-start | bytes 491528 | tf_op jit(solution)/shard_map/ppermute | solution.py:261
  69.2 26.9 %collective-permute-start.10 = (f32[320,128]{1,0:T(8,128)S(1)}, f32[320,128]{1,0:T(8,128)S(1)}, u32[]{:S(2)}, u32[]{:S(2)}) collective-permute-start(f32[320,128]{1,0:T(8,128)S(1)} %get-tuple-element.34), channel_id=1, source_target_pairs={{0,128},{32,160},{64,192},{96,224},{128,0},{160,32},{192,64},{224,... | collective-permute-start | bytes 491528 | tf_op jit(solution)/shard_map/ppermute | solution.py:261
  73.9 22.2 %collective-permute-start.11 = (f32[320,128]{1,0:T(8,128)S(1)}, f32[320,128]{1,0:T(8,128)S(1)}, u32[]{:S(2)}, u32[]{:S(2)}) collective-permute-start(f32[320,128]{1,0:T(8,128)S(1)} %get-tuple-element.35), channel_id=1, source_target_pairs={{0,160},{32,192},{64,224},{96,0},{128,32},{160,64},{192,96},{224,1... | collective-permute-start | bytes 491528 | tf_op jit(solution)/shard_map/ppermute | solution.py:261
  75.4 24.2 %collective-permute-start.12 = (f32[320,128]{1,0:T(8,128)}, f32[320,128]{1,0:T(8,128)S(1)}, u32[]{:S(2)}, u32[]{:S(2)}) collective-permute-start(f32[320,128]{1,0:T(8,128)} %get-tuple-element.36), channel_id=1, source_target_pairs={{0,192},{32,224},{64,0},{96,32},{128,64},{160,96},{192,128},{224,1... | collective-permute-start | bytes 491528 | tf_op jit(solution)/shard_map/ppermute | solution.py:261
  84.5 18.6 %collective-permute-start.13 = (f32[320,128]{1,0:T(8,128)}, f32[320,128]{1,0:T(8,128)S(1)}, u32[]{:S(2)}, u32[]{:S(2)}) collective-permute-start(f32[320,128]{1,0:T(8,128)} %get-tuple-element.37), channel_id=1, source_target_pairs={{0,224},{32,0},{64,32},{96,64},{128,96},{160,128},{192,160},{224,1... | collective-permute-start | bytes 491528 | tf_op jit(solution)/shard_map/ppermute | solution.py:261

commit v5 on v4

--- a/solution.py
+++ b/solution.py
@@ -114,27 +114,31 @@
                 spec[h, pl.ds(N, N), :] = q[N:, one] + q[:N, two]
         for b in bands:
             turn(b, 0)
-    for b in range(BANDS):
+    for z in range(ZD):
         for yh in range(2):
-            for z in range(ZD):
-                one_ref[pl.ds(hops[z] * PIECE + 8 * PLANE + yh * PLANE + b, 4, stride=COLS), :] = spec[
-                    yh, pl.ds(z * 32 + b, 4, stride=8), :
-                ]
+            for r in range(4):
+                row = hops[z] * PIECE + 8 * PLANE + yh * PLANE + r * 8
+                one_ref[pl.ds(pl.multiple_of(row, 8), 8), :] = spec[yh, pl.ds(z * 32 + r * 8, 8), :]
     out = [
         pltpu.make_async_copy(one_ref.at[pl.ds(k * PIECE, PIECE)], out_one[k], sems.at[4 + 2 * BANDS + k])
         for k in range(ZD)
     ]
     for copy in out:
         copy.start()
+    for z in range(ZD):
+        for yh in range(2):
+            for r in range(4):
+                two_ref[pl.ds(r * COLS * SLOT + 8 * ZD + hops[z] * 2 + yh, 8, stride=SLOT), :] = spec[
+                    yh, pl.ds(N + z * 32 + r * 8, 8), :
+                ]
     for b in range(BANDS):
         turn(b, 1)
-        for yh in range(2):
-            for z in range(ZD):
-                two_ref[pl.ds(b * SLOT + 8 * ZD + hops[z] * 2 + yh, 4, stride=COLS * SLOT), :] = spec[
-                    yh, pl.ds(N + z * 32 + b, 4, stride=8), :
-                ]
-    out.append(pltpu.make_async_copy(two_ref, out_two, sems.at[4 + 2 * BANDS + ZD]))
-    out[-1].start()
+        for r in range(4):
+            where = pl.ds((r * COLS + b) * SLOT, SLOT)
+            out.append(
+                pltpu.make_async_copy(two_ref.at[where], out_two.at[where], sems.at[4 + 2 * BANDS + ZD + 4 * b + r])
+            )
+            out[-1].start()
     for copy in out:
         copy.wait()
 
@@ -164,15 +168,21 @@
 
 
 def join(*refs):
-    *in_refs, out_ref = refs
-    for k, in_ref in enumerate(in_refs):
-        for p in range(PLANE):
-            out_ref[pl.ds(p * SLOT + k * 8, 8), :] = in_ref[pl.ds(p * 8, 8), :]
-        for j in range(2):
-            for g in range(PLANE // 8):
-                out_ref[pl.ds(g * 8 * SLOT + 8 * ZD + k * 2 + j, 8, stride=SLOT), :] = in_ref[
+    *in_refs, out_ref, held, sems = refs
+    copies = []
+    for g in range(PLANE // 8):
+        for k, in_ref in enumerate(in_refs):
+            for p in range(g * 8, g * 8 + 8):
+                held[pl.ds(p * SLOT + k * 8, 8), :] = in_ref[pl.ds(p * 8, 8), :]
+            for j in range(2):
+                held[pl.ds(g * 8 * SLOT + 8 * ZD + k * 2 + j, 8, stride=SLOT), :] = in_ref[
                     pl.ds(PLANE * 8 + j * PLANE + g * 8, 8), :
                 ]
+        where = pl.ds(g * 8 * SLOT, 8 * SLOT)
+        copies.append(pltpu.make_async_copy(held.at[where], out_ref.at[where], sems.at[g]))
+        copies[-1].start()
+    for copy in copies:
+        copy.wait()
 
 
 BEFORE = 6
@@ -285,7 +295,7 @@
             pltpu.VMEM((2 * N, N), bf16),
             pltpu.VMEM((2 * N, N), bf16),
             pltpu.VMEM((2, 2 * N, LANES), f32),
-            pltpu.SemaphoreType.DMA((5 + 2 * BANDS + ZD,)),
+            pltpu.SemaphoreType.DMA((4 + 6 * BANDS + ZD,)),
         ],
         compiler_params=params,
     )(
@@ -312,9 +322,13 @@
     one = pl.pallas_call(
         join,
         name="join",
-        out_shape=jax.ShapeDtypeStruct((ZD * PIECE, LANES), f32),
+        out_shape=pltpu.HBM((PLANE * SLOT, LANES), f32),
         in_specs=[vmem] * ZD,
-        out_specs=vmem,
+        out_specs=anywhere,
+        scratch_shapes=[
+            pltpu.VMEM((PLANE * SLOT, LANES), f32),
+            pltpu.SemaphoreType.DMA((PLANE // 8,)),
+        ],
         compiler_params=params,
     )(*one)
     one = one.reshape(PLANE, SLOT, LANES)

time: 109 us -> 109 us (level)
  transfers between devices with their start and end apart: 16 -> 16, of which waited for: 10 -> 10; matrix products, arithmetic and copies ran while one was open for 0% -> 0% of each run, Pallas kernels for 1% -> 2%
where the time goes in v5:
time: 109 us; the launch traced here: 108 us
  starting transfers between devices  49.2 us (45%)
  waiting for transfers between devices  44.8 us (41%)
  Pallas kernels  13.1 us (12%)
    ppermute x14, waiting for transfers between devices, by_hop(): out[k] = lax.ppermute(values[k], 'z', shift[k])  44.8 us
    ppermute x14, starting transfers between devices, by_hop(): out[k] = lax.ppermute(values[k], 'z', shift[k])  34.2 us
    all_to_all x1, starting transfers between devices, local(): lax.all_to_all(two.reshape(PLANE, SLOT, LANES), plane, split_axis=0, conc...  7.55 us
    all_to_all x1, starting transfers between devices, local(): one = lax.all_to_all(one, plane, split_axis=0, concat_axis=0, tiled=True)  7.43 us
    pallas_call x1, Pallas kernels, local(): pl.pallas_call(pack, name='pack', out_shape=[jax.ShapeDtypeStruct((PIECE,...  6.24 us
    pallas_call x1, Pallas kernels, local(): pl.pallas_call(unpack, name='unpack', out_shape=[jax.ShapeDtypeStruct((4...  4.77 us
  transfers between devices with their start and end apart: 16, of which 10 were waited for; matrix products, arithmetic and copies ran while one was open for 0% of the time, Pallas kernels for 2%

profile of v5, /device:TPU:8, one launch (start us, length us, event | category | flops | bytes accessed | tf_op | source)
XLA Modules:
  0.0 107.9 jit_solution(8851712568225836500)
XLA Ops:
  0.6 6.2 %pack.1 = (f32[320,128]{1,0:T(8,128)S(1)}, f32[320,128]{1,0:T(8,128)S(1)}, f32[320,128]{1,0:T(8,128)S(1)}, f32[320,128]{1,0:T(8,128)S(1)}, f32[320,128]{1,0:T(8,...) custom-call(f32[512,256]{1,0:T(8,128)} %bitcast.12, ...), custom_call_target="tpu_custom_call" | custom-call | tf_op jit(solution)/shard_map/pack/pallas_call | solution.py:284
  6.9 7.5 %all-to-all-start.1 = ((f32[32,80,128]{2,1,0:T(8,128)}), f32[32,80,128]{2,1,0:T(8,128)S(1)}, u32[]{:S(2)}, u32[]{:S(2)}) async-start(f32[32,80,128]{2,1,0:T(8,128)} %bitcast.4), calls=%async_computation.1 | async-start | bytes 2621440 | tf_op jit(solution)/shard_map/all_to_all | solution.py:307
  14.4 2.0 %collective-permute-start = (f32[320,128]{1,0:T(8,128)S(1)}, f32[320,128]{1,0:T(8,128)S(1)}, u32[]{:S(2)}, u32[]{:S(2)}) collective-permute-start(f32[320,128]{1,0:T(8,128)S(1)} %get-tuple-element.22), channel_id=1, source_target_pairs={{0,32},{32,64},{64,96},{96,128},{128,160},{160,192},{192,224},{224... | collective-permute-start | bytes 491528 | tf_op jit(solution)/shard_map/ppermute | solution.py:271
  16.4 3.3 %collective-permute-start.1 = (f32[320,128]{1,0:T(8,128)S(1)}, f32[320,128]{1,0:T(8,128)S(1)}, u32[]{:S(2)}, u32[]{:S(2)}) collective-permute-start(f32[320,128]{1,0:T(8,128)S(1)} %get-tuple-element.23), channel_id=1, source_target_pairs={{0,64},{32,96},{64,128},{96,160},{128,192},{160,224},{192,0},{224,... | collective-permute-start | bytes 491528 | tf_op jit(solution)/shard_map/ppermute | solution.py:271
  19.7 4.0 %collective-permute-start.2 = (f32[320,128]{1,0:T(8,128)S(1)}, f32[320,128]{1,0:T(8,128)S(1)}, u32[]{:S(2)}, u32[]{:S(2)}) collective-permute-start(f32[320,128]{1,0:T(8,128)S(1)} %get-tuple-element.24), channel_id=1, source_target_pairs={{0,96},{32,128},{64,160},{96,192},{128,224},{160,0},{192,32},{224,... | collective-permute-start | bytes 491528 | tf_op jit(solution)/shard_map/ppermute | solution.py:271
  23.7 0.5 collective-permute-start.3
  24.3 4.9 %collective-permute-start.4 = (f32[320,128]{1,0:T(8,128)S(1)}, f32[320,128]{1,0:T(8,128)S(1)}, u32[]{:S(2)}, u32[]{:S(2)}) collective-permute-start(f32[320,128]{1,0:T(8,128)S(1)} %get-tuple-element.26), channel_id=1, source_target_pairs={{0,160},{32,192},{64,224},{96,0},{128,32},{160,64},{192,96},{224,1... | collective-permute-start | bytes 491528 | tf_op jit(solution)/shard_map/ppermute | solution.py:271
  29.2 0.0 collective-permute-done.refs_1_
  29.2 2.7 %collective-permute-start.5 = (f32[320,128]{1,0:T(8,128)S(1)}, f32[320,128]{1,0:T(8,128)S(1)}, u32[]{:S(2)}, u32[]{:S(2)}) collective-permute-start(f32[320,128]{1,0:T(8,128)S(1)} %get-tuple-element.27), channel_id=1, source_target_pairs={{0,192},{32,224},{64,0},{96,32},{128,64},{160,96},{192,128},{224,1... | collective-permute-start | bytes 491528 | tf_op jit(solution)/shard_map/ppermute | solution.py:271
  31.9 3.2 %collective-permute-done.1.refs_2_ = f32[320,128]{1,0:T(8,128)S(1)} collective-permute-done((f32[320,128]{1,0:T(8,128)S(1)}, f32[320,128]{1,0:T(8,128)S(1)}, u32[]{:S(2)}, u32[]{:S(2)}) %collective-permute-start.1) | collective-permute-done | bytes 163872 | tf_op jit(solution)/shard_map/ppermute | solution.py:271
  35.1 2.6 %collective-permute-start.6 = (f32[320,128]{1,0:T(8,128)S(1)}, f32[320,128]{1,0:T(8,128)S(1)}, u32[]{:S(2)}, u32[]{:S(2)}) collective-permute-start(f32[320,128]{1,0:T(8,128)S(1)} %get-tuple-element.28), channel_id=1, source_target_pairs={{0,224},{32,0},{64,32},{96,64},{128,96},{160,128},{192,160},{224,1... | collective-permute-start | bytes 491528 | tf_op jit(solution)/shard_map/ppermute | solution.py:271
  37.7 8.5 %collective-permute-done.2.refs_3_ = f32[320,128]{1,0:T(8,128)S(1)} collective-permute-done((f32[320,128]{1,0:T(8,128)S(1)}, f32[320,128]{1,0:T(8,128)S(1)}, u32[]{:S(2)}, u32[]{:S(2)}) %collective-permute-start.2) | collective-permute-done | bytes 163872 | tf_op jit(solution)/shard_map/ppermute | solution.py:271
  46.1 0.0 collective-permute-done.3.refs_4_
  46.1 2.2 %collective-permute-done.4.refs_5_ = f32[320,128]{1,0:T(8,128)S(1)} collective-permute-done((f32[320,128]{1,0:T(8,128)S(1)}, f32[320,128]{1,0:T(8,128)S(1)}, u32[]{:S(2)}, u32[]{:S(2)}) %collective-permute-start.4) | collective-permute-done | bytes 163872 | tf_op jit(solution)/shard_map/ppermute | solution.py:271
  48.3 4.8 %collective-permute-done.5.refs_6_ = f32[320,128]{1,0:T(8,128)S(1)} collective-permute-done((f32[320,128]{1,0:T(8,128)S(1)}, f32[320,128]{1,0:T(8,128)S(1)}, u32[]{:S(2)}, u32[]{:S(2)}) %collective-permute-start.5) | collective-permute-done | bytes 163872 | tf_op jit(solution)/shard_map/ppermute | solution.py:271
  53.1 1.1 %collective-permute-done.6.refs_7_ = f32[320,128]{1,0:T(8,128)S(1)} collective-permute-done((f32[320,128]{1,0:T(8,128)S(1)}, f32[320,128]{1,0:T(8,128)S(1)}, u32[]{:S(2)}, u32[]{:S(2)}) %collective-permute-start.6) | collective-permute-done | bytes 163872 | tf_op jit(solution)/shard_map/ppermute | solution.py:271
  54.2 1.2 %join.1 = f32[2560,128]{1,0:T(8,128)} custom-call(f32[320,128]{1,0:T(8,128)S(1)} %get-tuple-element.21.refs_0_, f32[320,128]{1,0:T(8,128)S(1)} %collective-permute-done.refs_1_, f32[320,128]{1,0:T(8,128)S(1)} %collective-permute-done.1.refs_2_, f32[320,128]{1,0:T(8,128)S(1)} %collective-permute-done.2.refs_3_, ...), custom_call_target="tpu_custom_call" | custom-call | tf_op jit(solution)/shard_map/join/pallas_call | solution.py:322
  55.4 0.0 all-to-all-done.1
  55.4 7.4 %all-to-all-start = ((f32[32,80,128]{2,1,0:T(8,128)}), f32[32,80,128]{2,1,0:T(8,128)S(1)}, u32[]{:S(2)}, u32[]{:S(2)}) async-start(f32[32,80,128]{2,1,0:T(8,128)} %bitcast.10), calls=%async_computation | async-start | bytes 2621440 | tf_op jit(solution)/shard_map/all_to_all | solution.py:335
  62.8 0.9 regroup.1
  63.7 3.6 %collective-permute-start.7 = (f32[320,128]{1,0:T(8,128)}, f32[320,128]{1,0:T(8,128)S(1)}, u32[]{:S(2)}, u32[]{:S(2)}) collective-permute-start(f32[320,128]{1,0:T(8,128)} %get-tuple-element.31), channel_id=1, source_target_pairs={{0,32},{32,64},{64,96},{96,128},{128,160},{160,192},{192,224},{224... | collective-permute-start | bytes 491528 | tf_op jit(solution)/shard_map/ppermute | solution.py:271
  67.4 1.1 %collective-permute-start.8 = (f32[320,128]{1,0:T(8,128)}, f32[320,128]{1,0:T(8,128)S(1)}, u32[]{:S(2)}, u32[]{:S(2)}) collective-permute-start(f32[320,128]{1,0:T(8,128)} %get-tuple-element.32), channel_id=1, source_target_pairs={{0,64},{32,96},{64,128},{96,160},{128,192},{160,224},{192,0},{224,... | collective-permute-start | bytes 491528 | tf_op jit(solution)/shard_map/ppermute | solution.py:271
  68.5 0.6 collective-permute-start.9
  69.1 4.7 %collective-permute-start.10 = (f32[320,128]{1,0:T(8,128)S(1)}, f32[320,128]{1,0:T(8,128)S(1)}, u32[]{:S(2)}, u32[]{:S(2)}) collective-permute-start(f32[320,128]{1,0:T(8,128)S(1)} %get-tuple-element.34), channel_id=1, source_target_pairs={{0,128},{32,160},{64,192},{96,224},{128,0},{160,32},{192,64},{224,... | collective-permute-start | bytes 491528 | tf_op jit(solution)/shard_map/ppermute | solution.py:271
  73.8 1.5 %collective-permute-start.11 = (f32[320,128]{1,0:T(8,128)S(1)}, f32[320,128]{1,0:T(8,128)S(1)}, u32[]{:S(2)}, u32[]{:S(2)}) collective-permute-start(f32[320,128]{1,0:T(8,128)S(1)} %get-tuple-element.35), channel_id=1, source_target_pairs={{0,160},{32,192},{64,224},{96,0},{128,32},{160,64},{192,96},{224,1... | collective-permute-start | bytes 491528 | tf_op jit(solution)/shard_map/ppermute | solution.py:271
  75.3 0.0 collective-permute-done.7.refs_2_
  75.3 2.4 %collective-permute-start.12 = (f32[320,128]{1,0:T(8,128)}, f32[320,128]{1,0:T(8,128)S(1)}, u32[]{:S(2)}, u32[]{:S(2)}) collective-permute-start(f32[320,128]{1,0:T(8,128)} %get-tuple-element.36), channel_id=1, source_target_pairs={{0,192},{32,224},{64,0},{96,32},{128,64},{160,96},{192,128},{224,1... | collective-permute-start | bytes 491528 | tf_op jit(solution)/shard_map/ppermute | solution.py:271
  77.7 5.6 %collective-permute-done.8.refs_3_ = f32[320,128]{1,0:T(8,128)S(1)} collective-permute-done((f32[320,128]{1,0:T(8,128)}, f32[320,128]{1,0:T(8,128)S(1)}, u32[]{:S(2)}, u32[]{:S(2)}) %collective-permute-start.8) | collective-permute-done | bytes 163872 | tf_op jit(solution)/shard_map/ppermute | solution.py:271
  83.3 0.2 collective-permute-start.13
  83.5 6.4 %collective-permute-done.9.refs_4_ = f32[320,128]{1,0:T(8,128)S(1)} collective-permute-done((f32[320,128]{1,0:T(8,128)S(1)}, f32[320,128]{1,0:T(8,128)S(1)}, u32[]{:S(2)}, u32[]{:S(2)}) %collective-permute-start.9) | collective-permute-done | bytes 163872 | tf_op jit(solution)/shard_map/ppermute | solution.py:271
  89.9 5.6 %collective-permute-done.10.refs_5_ = f32[320,128]{1,0:T(8,128)S(1)} collective-permute-done((f32[320,128]{1,0:T(8,128)S(1)}, f32[320,128]{1,0:T(8,128)S(1)}, u32[]{:S(2)}, u32[]{:S(2)}) %collective-permute-start.10) | collective-permute-done | bytes 163872 | tf_op jit(solution)/shard_map/ppermute | solution.py:271
  95.5 0.0 collective-permute-done.11.refs_6_
  95.5 4.0 %collective-permute-done.12.refs_7_ = f32[320,128]{1,0:T(8,128)S(1)} collective-permute-done((f32[320,128]{1,0:T(8,128)}, f32[320,128]{1,0:T(8,128)S(1)}, u32[]{:S(2)}, u32[]{:S(2)}) %collective-permute-start.12) | collective-permute-done | bytes 163872 | tf_op jit(solution)/shard_map/ppermute | solution.py:271
  99.5 3.5 %collective-permute-done.13.refs_8_ = f32[320,128]{1,0:T(8,128)S(1)} collective-permute-done((f32[320,128]{1,0:T(8,128)}, f32[320,128]{1,0:T(8,128)S(1)}, u32[]{:S(2)}, u32[]{:S(2)}) %collective-permute-start.13) | collective-permute-done | bytes 163872 | tf_op jit(solution)/shard_map/ppermute | solution.py:271
  103.0 0.0 all-to-all-done
  103.0 4.8 %unpack.1 = (f32[1024,128]{1,0:T(8,128)}, f32[8,256,256]{2,1,0:T(8,128)}) custom-call(f32[2560,128]{1,0:T(8,128)S(1)} %bitcast.8, f32[320,128]{1,0:T(8,128)S(1)} %get-tuple-element.30.refs_1_, f32[320,128]{1,0:T(8,128)S(1)} %collective-permute-done.7.refs_2_, f32[320,128]{1,0:T(8,128)S(1)} %collective-permute-done.8.refs_3_, ...), custom_call_target="tpu_custom_call" | custom-call | tf_op jit(solution)/shard_map/unpack/pallas_call | solution.py:336
Async XLA Ops:
  6.9 48.5 %all-to-all-start.1 = ((f32[32,80,128]{2,1,0:T(8,128)}), f32[32,80,128]{2,1,0:T(8,128)S(1)}, u32[]{:S(2)}, u32[]{:S(2)}) async-start(f32[32,80,128]{2,1,0:T(8,128)} %bitcast.4), calls=%async_computation.1 | async-start | bytes 2621440 | tf_op jit(solution)/shard_map/all_to_all | solution.py:307
  14.4 14.8 %collective-permute-start = (f32[320,128]{1,0:T(8,128)S(1)}, f32[320,128]{1,0:T(8,128)S(1)}, u32[]{:S(2)}, u32[]{:S(2)}) collective-permute-start(f32[320,128]{1,0:T(8,128)S(1)} %get-tuple-element.22), channel_id=1, source_target_pairs={{0,32},{32,64},{64,96},{96,128},{128,160},{160,192},{192,224},{224... | collective-permute-start | bytes 491528 | tf_op jit(solution)/shard_map/ppermute | solution.py:271
  16.4 18.6 %collective-permute-start.1 = (f32[320,128]{1,0:T(8,128)S(1)}, f32[320,128]{1,0:T(8,128)S(1)}, u32[]{:S(2)}, u32[]{:S(2)}) collective-permute-start(f32[320,128]{1,0:T(8,128)S(1)} %get-tuple-element.23), channel_id=1, source_target_pairs={{0,64},{32,96},{64,128},{96,160},{128,192},{160,224},{192,0},{224,... | collective-permute-start | bytes 491528 | tf_op jit(solution)/shard_map/ppermute | solution.py:271
  19.7 26.4 %collective-permute-start.2 = (f32[320,128]{1,0:T(8,128)S(1)}, f32[320,128]{1,0:T(8,128)S(1)}, u32[]{:S(2)}, u32[]{:S(2)}) collective-permute-start(f32[320,128]{1,0:T(8,128)S(1)} %get-tuple-element.24), channel_id=1, source_target_pairs={{0,96},{32,128},{64,160},{96,192},{128,224},{160,0},{192,32},{224,... | collective-permute-start | bytes 491528 | tf_op jit(solution)/shard_map/ppermute | solution.py:271
  23.7 22.4 %collective-permute-start.3 = (f32[320,128]{1,0:T(8,128)S(1)}, f32[320,128]{1,0:T(8,128)S(1)}, u32[]{:S(2)}, u32[]{:S(2)}) collective-permute-start(f32[320,128]{1,0:T(8,128)S(1)} %get-tuple-element.25), channel_id=1, source_target_pairs={{0,128},{32,160},{64,192},{96,224},{128,0},{160,32},{192,64},{224,... | collective-permute-start | bytes 491528 | tf_op jit(solution)/shard_map/ppermute | solution.py:271
  24.3 24.0 %collective-permute-start.4 = (f32[320,128]{1,0:T(8,128)S(1)}, f32[320,128]{1,0:T(8,128)S(1)}, u32[]{:S(2)}, u32[]{:S(2)}) collective-permute-start(f32[320,128]{1,0:T(8,128)S(1)} %get-tuple-element.26), channel_id=1, source_target_pairs={{0,160},{32,192},{64,224},{96,0},{128,32},{160,64},{192,96},{224,1... | collective-permute-start | bytes 491528 | tf_op jit(solution)/shard_map/ppermute | solution.py:271
  29.2 23.9 %collective-permute-start.5 = (f32[320,128]{1,0:T(8,128)S(1)}, f32[320,128]{1,0:T(8,128)S(1)}, u32[]{:S(2)}, u32[]{:S(2)}) collective-permute-start(f32[320,128]{1,0:T(8,128)S(1)} %get-tuple-element.27), channel_id=1, source_target_pairs={{0,192},{32,224},{64,0},{96,32},{128,64},{160,96},{192,128},{224,1... | collective-permute-start | bytes 491528 | tf_op jit(solution)/shard_map/ppermute | solution.py:271
  35.1 19.2 %collective-permute-start.6 = (f32[320,128]{1,0:T(8,128)S(1)}, f32[320,128]{1,0:T(8,128)S(1)}, u32[]{:S(2)}, u32[]{:S(2)}) collective-permute-start(f32[320,128]{1,0:T(8,128)S(1)} %get-tuple-element.28), channel_id=1, source_target_pairs={{0,224},{32,0},{64,32},{96,64},{128,96},{160,128},{192,160},{224,1... | collective-permute-start | bytes 491528 | tf_op jit(solution)/shard_map/ppermute | solution.py:271
  55.4 47.6 %all-to-all-start = ((f32[32,80,128]{2,1,0:T(8,128)}), f32[32,80,128]{2,1,0:T(8,128)S(1)}, u32[]{:S(2)}, u32[]{:S(2)}) async-start(f32[32,80,128]{2,1,0:T(8,128)} %bitcast.10), calls=%async_computation | async-start | bytes 2621440 | tf_op jit(solution)/shard_map/all_to_all | solution.py:335
  63.7 11.6 %collective-permute-start.7 = (f32[320,128]{1,0:T(8,128)}, f32[320,128]{1,0:T(8,128)S(1)}, u32[]{:S(2)}, u32[]{:S(2)}) collective-permute-start(f32[320,128]{1,0:T(8,128)} %get-tuple-element.31), channel_id=1, source_target_pairs={{0,32},{32,64},{64,96},{96,128},{128,160},{160,192},{192,224},{224... | collective-permute-start | bytes 491528 | tf_op jit(solution)/shard_map/ppermute | solution.py:271
  67.4 15.9 %collective-permute-start.8 = (f32[320,128]{1,0:T(8,128)}, f32[320,128]{1,0:T(8,128)S(1)}, u32[]{:S(2)}, u32[]{:S(2)}) collective-permute-start(f32[320,128]{1,0:T(8,128)} %get-tuple-element.32), channel_id=1, source_target_pairs={{0,64},{32,96},{64,128},{96,160},{128,192},{160,224},{192,0},{224,... | collective-permute-start | bytes 491528 | tf_op jit(solution)/shard_map/ppermute | solution.py:271
  68.5 21.4 %collective-permute-start.9 = (f32[320,128]{1,0:T(8,128)S(1)}, f32[320,128]{1,0:T(8,128)S(1)}, u32[]{:S(2)}, u32[]{:S(2)}) collective-permute-start(f32[320,128]{1,0:T(8,128)S(1)} %get-tuple-element.33), channel_id=1, source_target_pairs={{0,96},{32,128},{64,160},{96,192},{128,224},{160,0},{192,32},{224,... | collective-permute-start | bytes 491528 | tf_op jit(solution)/shard_map/ppermute | solution.py:271
  69.1 26.4 %collective-permute-start.10 = (f32[320,128]{1,0:T(8,128)S(1)}, f32[320,128]{1,0:T(8,128)S(1)}, u32[]{:S(2)}, u32[]{:S(2)}) collective-permute-start(f32[320,128]{1,0:T(8,128)S(1)} %get-tuple-element.34), channel_id=1, source_target_pairs={{0,128},{32,160},{64,192},{96,224},{128,0},{160,32},{192,64},{224,... | collective-permute-start | bytes 491528 | tf_op jit(solution)/shard_map/ppermute | solution.py:271
  73.8 21.7 %collective-permute-start.11 = (f32[320,128]{1,0:T(8,128)S(1)}, f32[320,128]{1,0:T(8,128)S(1)}, u32[]{:S(2)}, u32[]{:S(2)}) collective-permute-start(f32[320,128]{1,0:T(8,128)S(1)} %get-tuple-element.35), channel_id=1, source_target_pairs={{0,160},{32,192},{64,224},{96,0},{128,32},{160,64},{192,96},{224,1... | collective-permute-start | bytes 491528 | tf_op jit(solution)/shard_map/ppermute | solution.py:271
  75.3 24.2 %collective-permute-start.12 = (f32[320,128]{1,0:T(8,128)}, f32[320,128]{1,0:T(8,128)S(1)}, u32[]{:S(2)}, u32[]{:S(2)}) collective-permute-start(f32[320,128]{1,0:T(8,128)} %get-tuple-element.36), channel_id=1, source_target_pairs={{0,192},{32,224},{64,0},{96,32},{128,64},{160,96},{192,128},{224,1... | collective-permute-start | bytes 491528 | tf_op jit(solution)/shard_map/ppermute | solution.py:271
  83.3 19.7 %collective-permute-start.13 = (f32[320,128]{1,0:T(8,128)}, f32[320,128]{1,0:T(8,128)S(1)}, u32[]{:S(2)}, u32[]{:S(2)}) collective-permute-start(f32[320,128]{1,0:T(8,128)} %get-tuple-element.37), channel_id=1, source_target_pairs={{0,224},{32,0},{64,32},{96,64},{128,96},{160,128},{192,160},{224,1... | collective-permute-start | bytes 491528 | tf_op jit(solution)/shard_map/ppermute | solution.py:271
